TPU v7x, 128 devices: a whole 4x4x4 slice. The times are simulated.
128 devices in a mesh: wide: 16 (over x_hi, y, core), narrow: 8 (over z, x_lo).
Axes of the slice: x: 4 (x_hi: 2, x_lo: 2; x = x_hi * 2 + x_lo), y: 4, z: 4, core: 2. Of those that a mesh axis runs over, the one named last changes fastest.
Arguments:
- image: bfloat16 [2, 256, 256, 256], P(None, 'wide', 'narrow'), may hold values from -6 to 6
- deapodization: float32 [3, 256], replicated, may hold values from 0.5 to 2
- offsets: int32 [128, 16], P(('wide', 'narrow')), may hold values from 0 to 256
- cross_weight: bfloat16 [128, 16, 1536, 256], P(('wide', 'narrow')), may hold values from -0.375 to 0.375
- x_weight: bfloat16 [128, 16, 1536, 256], P(('wide', 'narrow')), may hold values from -0.375 to 0.375
Outputs:
- samples: float32 [128, 16, 2, 1536], P(('wide', 'narrow'))
Inputs may be any that keep to these rules, and one draw needn't show every extreme that they name: `offsets`: each entry is the first row, along the first frequency dimension, of a group's window of 256 rows in one slab.
All inputs are finite; a program needn't handle non-finite values.
Results may differ from a plain program's by a relative error of at most 0.007.
Values may be sent and summed in bfloat16 or wider, within the bound.
No kernel may reach another device: no remote copies, remote signals or barrier semaphores. Data moves between devices by JAX's collectives and lax.ppermute only.
A program may use at most 128 MiB of HBM per device.

v0:
```python
import math

import jax
import jax.numpy as jnp
from jax import lax
from jax.sharding import PartitionSpec as P

G = 512
KZ = 64
BX = 256
SAMP = 1536


def shifted(block, axis, distance):
    devices = range(lax.axis_size(axis))
    route = [((i - distance) % len(devices), i) for i in devices]
    return lax.ppermute(block, axis, route)


def block_table(out_rows, inputs, grid_size, lowest):
    frequency = jnp.arange(out_rows, dtype=jnp.int32) + lowest
    position = jnp.arange(inputs, dtype=jnp.int32) - inputs // 2
    phases = jnp.mod(frequency[:, None] * position[None, :], grid_size)
    angles = phases.astype(jnp.float32) * (2.0 * math.pi / grid_size)
    factor = 1.0 / math.sqrt(inputs)
    cosine = (jnp.cos(angles) * factor).astype(jnp.bfloat16)
    sine = (jnp.sin(angles) * factor).astype(jnp.bfloat16)
    real_rows = jnp.stack([cosine, sine], axis=1)
    imag_rows = jnp.stack([-sine, cosine], axis=1)
    return jnp.stack([real_rows, imag_rows], axis=0)


def window_samples(window_rows, cross_rows, window_gain):
    partial_value = jnp.einsum(
        "ms,qcs->cmq", cross_rows, window_rows, preferred_element_type=jnp.float32
    )
    return jnp.sum(partial_value * window_gain.astype(jnp.float32)[None], axis=-1)


def per_device(image, deapodization, offsets, cross_weight, x_weight):
    wide_count = lax.axis_size("wide")
    wide_index = lax.axis_index("wide")
    narrow_index = lax.axis_index("narrow")
    block_x = image.shape[1]
    block_y = image.shape[2]
    image_width = image.shape[3]
    scale_x = lax.dynamic_slice_in_dim(deapodization[0], wide_index * block_x, block_x)
    scale_y = lax.dynamic_slice_in_dim(deapodization[1], narrow_index * block_y, block_y)
    weighted = (
        image.astype(jnp.float32)
        * scale_x[None, :, None, None]
        * scale_y[None, None, :, None]
        * deapodization[2][None, None, None, :]
    ).astype(jnp.bfloat16)
    z_table = block_table(KZ, image_width, G, -(KZ // 2))
    band_data = (
        jnp.einsum("okcz,cxyz->xyko", z_table, weighted, preferred_element_type=jnp.float32)
        .astype(jnp.bfloat16)
        .reshape(block_x, block_y, 2 * KZ)
    )
    line_table = block_table(G, image_width, G, -(G // 2))
    pieces = lax.all_to_all(band_data, "narrow", split_axis=2, concat_axis=1, tiled=True)
    item_count = pieces.shape[0]
    band_depth = pieces.shape[2] // 2
    unpacked = pieces.reshape(item_count, image_width, band_depth, 2)
    product = jnp.einsum(
        "oqcy,xykc->xoqk", line_table, unpacked, preferred_element_type=jnp.float32
    )
    columns = product.astype(jnp.bfloat16).reshape(item_count, 2, G * band_depth)
    slab_lines = lax.all_to_all(columns, "wide", split_axis=2, concat_axis=0, tiled=True)

    def transform_rows(table_rows, source):
        product = jnp.einsum(
            "opcx,xcs->pos", table_rows, source, preferred_element_type=jnp.float32
        )
        return product.astype(jnp.bfloat16)

    def slab_samples(slab_data, slab_index):
        start_row = lax.dynamic_index_in_dim(offsets[0], slab_index, 0, False)
        cross_rows = lax.dynamic_index_in_dim(cross_weight[0], slab_index, 0, False)
        window_gain = lax.dynamic_index_in_dim(x_weight[0], slab_index, 0, False)
        part_table = block_table(BX, image_width, G, start_row - G // 2)
        window_rows = transform_rows(part_table, slab_data)
        return window_samples(window_rows, cross_rows, window_gain)

    def record(results, slab_data, slab_index):
        return lax.dynamic_update_index_in_dim(
            results, slab_samples(slab_data, slab_index), slab_index, 0
        )

    results = jnp.zeros((wide_count, 2, SAMP), jnp.float32)

    def one_hop(hop_count, carried):
        current, results = carried
        incoming = shifted(current, "wide", 1)
        results = record(results, current, jnp.mod(wide_index - hop_count, wide_count))
        return (incoming, results)

    current, results = lax.fori_loop(0, wide_count - 1, one_hop, (slab_lines, results))
    results = record(results, current, jnp.mod(wide_index - (wide_count - 1), wide_count))
    return results[None]


def solution(mesh):
    return jax.shard_map(
        per_device,
        mesh=mesh,
        in_specs=(
            P(None, "wide", "narrow", None),
            P(),
            P(("wide", "narrow"), None),
            P(("wide", "narrow"), None, None, None),
            P(("wide", "narrow"), None, None, None),
        ),
        out_specs=P(("wide", "narrow"), None, None, None),
        check_vma=False,
    )
```

profile of v0, /device:TPU:0, one launch (start us, length us, event | category | flops | bytes accessed | tf_op | source)
XLA Modules:
  0.0 233.1 jit_solution(9781454502633909628)
XLA Ops:
  6.9 6.4 %all-to-all-start = ((bf16[8,2,4096]{2,1,0:T(2,128)(2,1)}), bf16[8,2,4096]{2,1,0:T(2,128)(2,1)S(1)}, u32[]{:S(2)}, u32[]{:S(2)}) async-start(bf16[8,2,4096]{2,1,0:T(2,128)(2,1)} %reshape.794), calls=%async_computation | async-start | bytes 262144 | tf_op jit(solution)/shard_map/all_to_all | solution.py:62
  13.3 2.5 %multiply_convert_fusion.3 = (bf16[512,1,256]{2,0,1:T(8,128)(2,1)S(1)}, bf16[512,1,256]{2,0,1:T(8,128)(2,1)S(1)}) fusion(s32[256]{0:T(256)S(1)} %get-tuple-element.280, s32[512]{0:T(512)S(1)} %iota_add_fusion.2), kind=kLoop, calls=%fused_computation.67 | loop fusion | flops 2359296 | bytes 527360 | tf_op jit(solution)/shard_map/convert_element_type | solution.py:27
  15.8 2.2 fusion.55
  23.8 1.7 copy.35
  25.4 18.1 %copy.65 = bf16[16,2,4096]{0,1,2:T(2,128)(2,1)} copy(bf16[16,2,4096]{0,2,1:T(8,128)(2,1)S(1)} %bitcast.158) | data formatting | bytes 524288 | tf_op jit(solution)/shard_map/reshape | solution.py:69
  43.6 7.3 %reshape.796 = bf16[16,2,4096]{2,1,0:T(2,128)(2,1)} reshape(bf16[4096,2,16]{2,1,0:T(2,128)(2,1)} %bitcast.159) | data formatting | bytes 524288
  50.9 6.9 %all-to-all-start.1 = ((bf16[16,2,4096]{2,1,0:T(2,128)(2,1)}), bf16[16,2,4096]{2,1,0:T(2,128)(2,1)S(1)}, u32[]{:S(2)}, u32[]{:S(2)}) async-start(bf16[16,2,4096]{2,1,0:T(2,128)(2,1)} %reshape.796), calls=%async_computation.1 | async-start | bytes 524288 | tf_op jit(solution)/shard_map/all_to_all | solution.py:70
  59.6 7.7 %all-to-all-done.1 = bf16[16,2,4096]{2,1,0:T(2,128)(2,1)S(1)} async-done(((bf16[16,2,4096]{2,1,0:T(2,128)(2,1)}), bf16[16,2,4096]{2,1,0:T(2,128)(2,1)S(1)}, u32[]{:S(2)}, u32[]{:S(2)}) %all-to-all-start.1) | async-done | bytes 262176 | tf_op jit(solution)/shard_map/all_to_all | solution.py:70
  68.7 3.2 %copy.57 = bf16[16,2,16,256]{3,0,2,1:T(8,128)(2,1)} copy(bf16[16,2,16,256]{0,1,3,2:T(2,128)(2,1)S(1)} %bitcast.157) | data formatting | bytes 524288 | tf_op jit(solution)/shard_map/all_to_all | solution.py:70
  72.7 157.0 %while.18 = (s32[]{:T(128)}, bf16[256,2,256]{2,0,1:T(8,128)(2,1)}, f32[16,2,1536]{2,1,0:T(2,128)}, s32[]{:T(128)}, s32[1,16]{1,0:T(1,128)S(1)}, /*index=5*/bf16[...) while((s32[]{:T(128)}, bf16[256,2,256]{2,0,1:T(8,128)(2,1)}, ...), condition=%wide.region_2.3_spmd, body=%wide.region_0.2_spmd.sunk | while | flops 541914624 | bytes 11577676 | solution.py:99
  78.8 2.1 fusion.81
  81.5 1.6 collective-permute-done
  89.3 2.1 fusion.81
  99.8 2.1 fusion.81
  110.2 2.1 fusion.81
  112.9 1.6 collective-permute-done
  120.7 2.1 fusion.81
  123.4 1.6 collective-permute-done
  131.2 2.1 fusion.81
  141.6 2.1 fusion.81
  152.1 2.1 fusion.81
  162.6 2.1 fusion.81
  173.0 2.1 fusion.81
  175.7 1.6 collective-permute-done
  183.5 2.1 fusion.81
  194.0 2.1 fusion.81
  204.4 2.1 fusion.81
  214.9 2.1 fusion.81
  217.6 1.6 collective-permute-done
  225.4 2.1 fusion.81
  228.1 1.6 collective-permute-done
  229.7 2.8 %fusion.22 = f32[2,1536]{1,0:T(2,128)S(1)} fusion(f32[1536,256]{0,1:T(8,128)} %copy.42, bf16[1,16,1536,256]{3,2,1,0:T(8,128)(2,1)} %get-tuple-element.372, s32[]{:T(128)S(6)} %select_n.179, bf16[1,256,2,256]{3,1,2,0:T(8,128)(2,1)} %get-tuple-element.267, bf16[1,256,2,256]{3,1,2,0:T(8,128)(2,1)S(1)} %get-tuple-element.266, ...), kind=kOutput, calls=%fused_computation.35 | convolution fusion | flops 539620352 | bytes 3158020 | tf_op jit(solution)/shard_map/ms,qcs->cmq/dot_general | solution.py:34
  (203 shorter events, 132.1 us)
Async XLA Ops:
  6.9 15.4 %all-to-all-start = ((bf16[8,2,4096]{2,1,0:T(2,128)(2,1)}), bf16[8,2,4096]{2,1,0:T(2,128)(2,1)S(1)}, u32[]{:S(2)}, u32[]{:S(2)}) async-start(bf16[8,2,4096]{2,1,0:T(2,128)(2,1)} %reshape.794), calls=%async_computation | async-start | bytes 262144 | tf_op jit(solution)/shard_map/all_to_all | solution.py:62
  50.9 21.8 %copy-start = (s32[1,16]{1,0:T(1,128)S(1)}, s32[1,16]{1,0:T(1,128)}, u32[]{:S(2)}) copy-start(s32[1,16]{1,0:T(1,128)} %param.9) | copy-start | bytes 196
  50.9 16.4 %all-to-all-start.1 = ((bf16[16,2,4096]{2,1,0:T(2,128)(2,1)}), bf16[16,2,4096]{2,1,0:T(2,128)(2,1)S(1)}, u32[]{:S(2)}, u32[]{:S(2)}) async-start(bf16[16,2,4096]{2,1,0:T(2,128)(2,1)} %reshape.796), calls=%async_computation.1 | async-start | bytes 524288 | tf_op jit(solution)/shard_map/all_to_all | solution.py:70
  73.6 9.5 %collective-permute-start = (bf16[256,2,256]{2,0,1:T(8,128)(2,1)S(1)}, bf16[256,2,256]{2,0,1:T(8,128)(2,1)}, u32[]{:S(2)}, u32[]{:S(2)}) collective-permute-start(bf16[256,2,256]{2,0,1:T(8,128)(2,1)S(1)} %copy.73), channel_id=1, source_target_pairs={{120,0},{0,8},{8,16},{16,24},{24,32},{32,40},{40,48},{48,56},{56,6... | collective-permute-start | bytes 786440 | tf_op jit(solution)/shard_map/while/body/eval_jaxpr/ppermute | solution.py:17
  84.1 9.5 %collective-permute-start = (bf16[256,2,256]{2,0,1:T(8,128)(2,1)S(1)}, bf16[256,2,256]{2,0,1:T(8,128)(2,1)}, u32[]{:S(2)}, u32[]{:S(2)}) collective-permute-start(bf16[256,2,256]{2,0,1:T(8,128)(2,1)S(1)} %copy.73), channel_id=1, source_target_pairs={{120,0},{0,8},{8,16},{16,24},{24,32},{32,40},{40,48},{48,56},{56,6... | collective-permute-start | bytes 786440 | tf_op jit(solution)/shard_map/while/body/eval_jaxpr/ppermute | solution.py:17
  94.6 9.5 %collective-permute-start = (bf16[256,2,256]{2,0,1:T(8,128)(2,1)S(1)}, bf16[256,2,256]{2,0,1:T(8,128)(2,1)}, u32[]{:S(2)}, u32[]{:S(2)}) collective-permute-start(bf16[256,2,256]{2,0,1:T(8,128)(2,1)S(1)} %copy.73), channel_id=1, source_target_pairs={{120,0},{0,8},{8,16},{16,24},{24,32},{32,40},{40,48},{48,56},{56,6... | collective-permute-start | bytes 786440 | tf_op jit(solution)/shard_map/while/body/eval_jaxpr/ppermute | solution.py:17
  105.0 9.5 %collective-permute-start = (bf16[256,2,256]{2,0,1:T(8,128)(2,1)S(1)}, bf16[256,2,256]{2,0,1:T(8,128)(2,1)}, u32[]{:S(2)}, u32[]{:S(2)}) collective-permute-start(bf16[256,2,256]{2,0,1:T(8,128)(2,1)S(1)} %copy.73), channel_id=1, source_target_pairs={{120,0},{0,8},{8,16},{16,24},{24,32},{32,40},{40,48},{48,56},{56,6... | collective-permute-start | bytes 786440 | tf_op jit(solution)/shard_map/while/body/eval_jaxpr/ppermute | solution.py:17
  115.5 9.5 %collective-permute-start = (bf16[256,2,256]{2,0,1:T(8,128)(2,1)S(1)}, bf16[256,2,256]{2,0,1:T(8,128)(2,1)}, u32[]{:S(2)}, u32[]{:S(2)}) collective-permute-start(bf16[256,2,256]{2,0,1:T(8,128)(2,1)S(1)} %copy.73), channel_id=1, source_target_pairs={{120,0},{0,8},{8,16},{16,24},{24,32},{32,40},{40,48},{48,56},{56,6... | collective-permute-start | bytes 786440 | tf_op jit(solution)/shard_map/while/body/eval_jaxpr/ppermute | solution.py:17
  126.0 9.5 %collective-permute-start = (bf16[256,2,256]{2,0,1:T(8,128)(2,1)S(1)}, bf16[256,2,256]{2,0,1:T(8,128)(2,1)}, u32[]{:S(2)}, u32[]{:S(2)}) collective-permute-start(bf16[256,2,256]{2,0,1:T(8,128)(2,1)S(1)} %copy.73), channel_id=1, source_target_pairs={{120,0},{0,8},{8,16},{16,24},{24,32},{32,40},{40,48},{48,56},{56,6... | collective-permute-start | bytes 786440 | tf_op jit(solution)/shard_map/while/body/eval_jaxpr/ppermute | solution.py:17
  136.5 9.5 %collective-permute-start = (bf16[256,2,256]{2,0,1:T(8,128)(2,1)S(1)}, bf16[256,2,256]{2,0,1:T(8,128)(2,1)}, u32[]{:S(2)}, u32[]{:S(2)}) collective-permute-start(bf16[256,2,256]{2,0,1:T(8,128)(2,1)S(1)} %copy.73), channel_id=1, source_target_pairs={{120,0},{0,8},{8,16},{16,24},{24,32},{32,40},{40,48},{48,56},{56,6... | collective-permute-start | bytes 786440 | tf_op jit(solution)/shard_map/while/body/eval_jaxpr/ppermute | solution.py:17
  146.9 9.5 %collective-permute-start = (bf16[256,2,256]{2,0,1:T(8,128)(2,1)S(1)}, bf16[256,2,256]{2,0,1:T(8,128)(2,1)}, u32[]{:S(2)}, u32[]{:S(2)}) collective-permute-start(bf16[256,2,256]{2,0,1:T(8,128)(2,1)S(1)} %copy.73), channel_id=1, source_target_pairs={{120,0},{0,8},{8,16},{16,24},{24,32},{32,40},{40,48},{48,56},{56,6... | collective-permute-start | bytes 786440 | tf_op jit(solution)/shard_map/while/body/eval_jaxpr/ppermute | solution.py:17
  157.4 9.5 %collective-permute-start = (bf16[256,2,256]{2,0,1:T(8,128)(2,1)S(1)}, bf16[256,2,256]{2,0,1:T(8,128)(2,1)}, u32[]{:S(2)}, u32[]{:S(2)}) collective-permute-start(bf16[256,2,256]{2,0,1:T(8,128)(2,1)S(1)} %copy.73), channel_id=1, source_target_pairs={{120,0},{0,8},{8,16},{16,24},{24,32},{32,40},{40,48},{48,56},{56,6... | collective-permute-start | bytes 786440 | tf_op jit(solution)/shard_map/while/body/eval_jaxpr/ppermute | solution.py:17
  167.9 9.5 %collective-permute-start = (bf16[256,2,256]{2,0,1:T(8,128)(2,1)S(1)}, bf16[256,2,256]{2,0,1:T(8,128)(2,1)}, u32[]{:S(2)}, u32[]{:S(2)}) collective-permute-start(bf16[256,2,256]{2,0,1:T(8,128)(2,1)S(1)} %copy.73), channel_id=1, source_target_pairs={{120,0},{0,8},{8,16},{16,24},{24,32},{32,40},{40,48},{48,56},{56,6... | collective-permute-start | bytes 786440 | tf_op jit(solution)/shard_map/while/body/eval_jaxpr/ppermute | solution.py:17
  178.3 9.5 %collective-permute-start = (bf16[256,2,256]{2,0,1:T(8,128)(2,1)S(1)}, bf16[256,2,256]{2,0,1:T(8,128)(2,1)}, u32[]{:S(2)}, u32[]{:S(2)}) collective-permute-start(bf16[256,2,256]{2,0,1:T(8,128)(2,1)S(1)} %copy.73), channel_id=1, source_target_pairs={{120,0},{0,8},{8,16},{16,24},{24,32},{32,40},{40,48},{48,56},{56,6... | collective-permute-start | bytes 786440 | tf_op jit(solution)/shard_map/while/body/eval_jaxpr/ppermute | solution.py:17
  188.8 9.5 %collective-permute-start = (bf16[256,2,256]{2,0,1:T(8,128)(2,1)S(1)}, bf16[256,2,256]{2,0,1:T(8,128)(2,1)}, u32[]{:S(2)}, u32[]{:S(2)}) collective-permute-start(bf16[256,2,256]{2,0,1:T(8,128)(2,1)S(1)} %copy.73), channel_id=1, source_target_pairs={{120,0},{0,8},{8,16},{16,24},{24,32},{32,40},{40,48},{48,56},{56,6... | collective-permute-start | bytes 786440 | tf_op jit(solution)/shard_map/while/body/eval_jaxpr/ppermute | solution.py:17
  199.3 9.5 %collective-permute-start = (bf16[256,2,256]{2,0,1:T(8,128)(2,1)S(1)}, bf16[256,2,256]{2,0,1:T(8,128)(2,1)}, u32[]{:S(2)}, u32[]{:S(2)}) collective-permute-start(bf16[256,2,256]{2,0,1:T(8,128)(2,1)S(1)} %copy.73), channel_id=1, source_target_pairs={{120,0},{0,8},{8,16},{16,24},{24,32},{32,40},{40,48},{48,56},{56,6... | collective-permute-start | bytes 786440 | tf_op jit(solution)/shard_map/while/body/eval_jaxpr/ppermute | solution.py:17
  209.7 9.5 %collective-permute-start = (bf16[256,2,256]{2,0,1:T(8,128)(2,1)S(1)}, bf16[256,2,256]{2,0,1:T(8,128)(2,1)}, u32[]{:S(2)}, u32[]{:S(2)}) collective-permute-start(bf16[256,2,256]{2,0,1:T(8,128)(2,1)S(1)} %copy.73), channel_id=1, source_target_pairs={{120,0},{0,8},{8,16},{16,24},{24,32},{32,40},{40,48},{48,56},{56,6... | collective-permute-start | bytes 786440 | tf_op jit(solution)/shard_map/while/body/eval_jaxpr/ppermute | solution.py:17
  220.2 9.5 %collective-permute-start = (bf16[256,2,256]{2,0,1:T(8,128)(2,1)S(1)}, bf16[256,2,256]{2,0,1:T(8,128)(2,1)}, u32[]{:S(2)}, u32[]{:S(2)}) collective-permute-start(bf16[256,2,256]{2,0,1:T(8,128)(2,1)S(1)} %copy.73), channel_id=1, source_target_pairs={{120,0},{0,8},{8,16},{16,24},{24,32},{32,40},{40,48},{48,56},{56,6... | collective-permute-start | bytes 786440 | tf_op jit(solution)/shard_map/while/body/eval_jaxpr/ppermute | solution.py:17
where the time goes:
time: 235 us; the launch traced here: 233 us
  local copies, waits for them, and re-layouts  83.9 us (36%)
  other arithmetic  66.6 us (28%)
  matrix products  36 us (15%)
  waiting for transfers between devices  32.3 us (14%)
  starting transfers between devices  13.3 us (6%)
    dot_general x16, matrix products, window_samples(): jnp.einsum('ms,qcs->cmq', cross_rows, window_rows, preferred_element_type...  34.1 us
    ppermute x15, waiting for transfers between devices, shifted(): return lax.ppermute(block, axis, route)  24.6 us
    convert_element_type x18, other arithmetic, block_table(): sine = (jnp.sin(angles) * factor).astype(jnp.bfloat16)  23.3 us
    dynamic_slice x30, local copies, waits for them, and re-layouts, slab_samples(): window_gain = lax.dynamic_index_in_dim(x_weight[0], slab_index, 0, False)  22 us
    neg x18, other arithmetic, block_table(): imag_rows = jnp.stack([-sine, cosine], axis=1)  19.6 us
    reshape x1, local copies, waits for them, and re-layouts, per_device(): product.astype(jnp.bfloat16).reshape(item_count, 2, G * band_depth)  18.1 us
    another operation x15, local copies, waits for them, and re-layouts  14.3 us
    unnamed x6, local copies, waits for them, and re-layouts  10.2 us
  transfers between devices with their start and end apart: 17, of which 16 were waited for; matrix products, arithmetic and copies ran while one was open for 55% of the time, Pallas kernels for 0%

commit v1 on v0

v1 whole, which is shorter than its diff:
```python
import math

import jax
import jax.numpy as jnp
import numpy as np
from jax import lax
from jax.experimental import pallas as pl
from jax.experimental.pallas import tpu as pltpu
from jax.sharding import PartitionSpec as P

N = 256
G = 512
KZ = 64
SAMP = 1536
SLABS = 16
NARROW = 8
CHIPS = 8
XB = 16
YB = 32
ZB = KZ // NARROW


def trig(frequency, position):
    phase = np.mod(np.asarray(frequency, np.int64)[:, None] * np.asarray(position, np.int64)[None, :], G)
    angle = phase.astype(np.float32) * np.float32(2.0 * math.pi / G)
    factor = np.float32(1.0 / math.sqrt(N))
    return (np.cos(angle) * factor).astype(np.float32), (np.sin(angle) * factor).astype(np.float32)


def complex_table(cosine, sine):
    real = np.stack([cosine, sine], axis=1)
    imag = np.stack([-sine, cosine], axis=1)
    return np.stack([real, imag], axis=0)


def tables():
    position = np.arange(N) - N // 2
    z = complex_table(*trig(np.arange(KZ) - KZ // 2, position))
    z = z.reshape(2, NARROW, ZB, 2, N).transpose(3, 4, 2, 1, 0).reshape(2 * N, ZB * NARROW * 2)
    y = complex_table(*trig(np.arange(G) - G // 2, position))
    y = y.reshape(2, G, 2, NARROW, YB).transpose(0, 1, 3, 2, 4).reshape(2 * G, 2 * N)
    x = complex_table(*trig(np.arange(N) - G // 2, position)).reshape(2 * N, 2 * N)
    offset = np.arange(N + 8)
    pc, ps = trig(offset, position)
    phase = np.concatenate([pc, ps], axis=1) * np.float32(math.sqrt(N))
    as_bf16 = lambda t: jnp.asarray(t, jnp.float32).astype(jnp.bfloat16)
    return as_bf16(z), as_bf16(y), as_bf16(x), jnp.asarray(phase, jnp.float32)


def nt(a, b):
    return lax.dot_general(a, b, (((1,), (1,)), ((), ())), preferred_element_type=jnp.float32)


def band_kernel(scale_s, scale_v, image, z_table, out, rows):
    wide = lax.axis_index("wide")
    narrow = lax.axis_index("narrow")
    lane = lax.broadcasted_iota(jnp.int32, (YB, N), 1)
    row = lax.broadcasted_iota(jnp.int32, (YB, N), 0)
    picked = jnp.where(lane == row + narrow * YB, scale_v[1:2, :], 0.0)
    scale_y = jnp.sum(picked, axis=1, keepdims=True)
    scale_z = scale_v[2:3, :]
    for x in range(XB):
        scale_x = scale_s[0, wide * XB + x]
        for c in range(2):
            value = image[c, x].astype(jnp.float32) * scale_x * scale_y * scale_z
            rows[x * YB:(x + 1) * YB, c * N:(c + 1) * N] = value.astype(jnp.bfloat16)
    product = jnp.dot(rows[...], z_table[...], preferred_element_type=jnp.float32)
    part = [product[x * YB:(x + 1) * YB] for x in range(XB)]
    lanes = lax.broadcasted_iota(jnp.int32, (YB, 128), 1)
    for bit in range(4):
        d = 1 << bit
        low = (lanes & d) == 0
        for i in range(XB):
            if i & d:
                continue
            a, b = part[i], part[i | d]
            part[i] = jnp.where(low, a, pltpu.roll(b, d, 1))
            part[i | d] = jnp.where(low, pltpu.roll(a, 128 - d, 1), b)
    for g in range(2 * NARROW):
        value = part[g].astype(jnp.bfloat16)
        for chip in range(CHIPS):
            out[chip, g // 2, (g % 2) * YB:(g % 2 + 1) * YB, :] = value


def sample_kernel(offsets, mine, other, y_table, x_table, phase, cross_hbm, gain_hbm, out,
                  band, columns, cross, gain, cross_sem, gain_sem):
    for s in range(SLABS):
        pltpu.make_async_copy(cross_hbm.at[s], cross.at[s], cross_sem.at[s]).start()
        pltpu.make_async_copy(gain_hbm.at[s], gain.at[s], gain_sem.at[s]).start()
    core = lax.rem(lax.axis_index("wide"), 2)
    for side, source in ((core, mine), (1 - core, other)):
        for chip in range(CHIPS):
            turned = source[chip].T
            start = pl.multiple_of((2 * chip + side) * XB, XB)
            for k in range(ZB):
                band[k, pl.ds(start, XB), :] = turned[k * XB:(k + 1) * XB]
    for k in range(ZB):
        lines = nt(y_table[...], band[k])
        for part in range(4):
            piece = lines[part // 2 * G:(part // 2 + 1) * G, part % 2 * 128:(part % 2 + 1) * 128]
            columns[part, pl.ds(k, G, stride=ZB), :] = piece

    def slab(s, carry):
        turn = phase[pl.ds(offsets[0, s], 1), :]
        start = pl.multiple_of(s * N, N)
        turned = []
        for half in range(2):
            cosine = turn[:, half * 128:(half + 1) * 128]
            sine = turn[:, N + half * 128:N + (half + 1) * 128]
            real = columns[half, pl.ds(start, N), :]
            imag = columns[2 + half, pl.ds(start, N), :]
            turned.append((real * cosine + imag * sine).astype(jnp.bfloat16))
            turned.append((imag * cosine - real * sine).astype(jnp.bfloat16))
        turned = jnp.concatenate([turned[0], turned[2], turned[1], turned[3]], axis=1)
        window = nt(x_table[...], turned).astype(jnp.bfloat16)
        pltpu.make_async_copy(cross_hbm.at[s], cross.at[s], cross_sem.at[s]).wait()
        pltpu.make_async_copy(gain_hbm.at[s], gain.at[s], gain_sem.at[s]).wait()
        for t in range(SAMP // N):
            cut = slice(t * N, (t + 1) * N)
            partial = nt(window, cross[s, cut, :])
            weight = gain[s, cut, :].T.astype(jnp.float32)
            out[s, 0:1, cut] = jnp.sum(partial[:N] * weight, axis=0, keepdims=True)
            out[s, 1:2, cut] = jnp.sum(partial[N:] * weight, axis=0, keepdims=True)
        return carry

    lax.fori_loop(0, SLABS, slab, 0)


def per_device(image, deapodization, offsets, cross_weight, x_weight):
    z_table, y_table, x_table, phase = tables()
    vmem = pl.BlockSpec(memory_space=pltpu.VMEM)
    smem = pl.BlockSpec(memory_space=pltpu.SMEM)
    hbm = pl.BlockSpec(memory_space=pl.ANY)
    band = pl.pallas_call(
        band_kernel,
        out_shape=jax.ShapeDtypeStruct((CHIPS, NARROW, 2 * YB, 128), jnp.bfloat16),
        in_specs=[smem, vmem, vmem, vmem],
        out_specs=vmem,
        scratch_shapes=[pltpu.VMEM((XB * YB, 2 * N), jnp.bfloat16)],
        name="band",
    )(deapodization, deapodization, image, z_table)
    groups = [[(chip * 2 + core) * NARROW + n for chip in range(CHIPS) for n in range(NARROW)]
              for core in range(2)]
    mine = lax.all_to_all(band.reshape(CHIPS * NARROW, 2 * YB, 128), ("wide", "narrow"), 0, 0,
                          axis_index_groups=groups, tiled=True)
    other = lax.ppermute(mine, "wide", [(i, i ^ 1) for i in range(2 * CHIPS)])
    result = pl.pallas_call(
        sample_kernel,
        out_shape=jax.ShapeDtypeStruct((SLABS, 2, SAMP), jnp.float32),
        in_specs=[smem, vmem, vmem, vmem, vmem, vmem, hbm, hbm],
        out_specs=vmem,
        scratch_shapes=[
            pltpu.VMEM((ZB, N, 2 * N), jnp.bfloat16),
            pltpu.VMEM((4, G * ZB, 128), jnp.float32),
            pltpu.VMEM((SLABS, SAMP, N), jnp.bfloat16),
            pltpu.VMEM((SLABS, SAMP, N), jnp.bfloat16),
            pltpu.SemaphoreType.DMA((SLABS,)),
            pltpu.SemaphoreType.DMA((SLABS,)),
        ],
        compiler_params=pltpu.CompilerParams(vmem_limit_bytes=60 * 1024 * 1024),
        name="samples",
    )(offsets, mine.reshape(CHIPS, NARROW * 2 * YB, 128), other.reshape(CHIPS, NARROW * 2 * YB, 128),
      y_table, x_table, phase, cross_weight[0], x_weight[0])
    return result[None]


def solution(mesh):
    return jax.shard_map(
        per_device,
        mesh=mesh,
        in_specs=(
            P(None, "wide", "narrow", None),
            P(),
            P(("wide", "narrow"), None),
            P(("wide", "narrow"), None, None, None),
            P(("wide", "narrow"), None, None, None),
        ),
        out_specs=P(("wide", "narrow"), None, None, None),
        check_vma=False,
    )
```

time: 235 us -> 62.6 us (0.27)
  the two profiles are of different devices: /device:TPU:0 before, /device:TPU:1 now
where the time goes in v1:
time: 62.6 us; the launch traced here: 62.3 us
  blocking collectives  28.3 us (45%)
  Pallas kernels  28.2 us (45%)
  starting transfers between devices  2.52 us (4%)
  waiting for transfers between devices  2.29 us (4%)
  local copies, waits for them, and re-layouts  1.02 us (2%)
    all_to_all x1, blocking collectives, per_device(): lax.all_to_all(band.reshape(CHIPS * NARROW, 2 * YB, 128), ('wide', 'narro...  28.3 us
    pallas_call x1, Pallas kernels, per_device(): pl.pallas_call(sample_kernel, out_shape=jax.ShapeDtypeStruct((SLABS, 2, S...  25.5 us
    pallas_call x1, Pallas kernels, per_device(): pl.pallas_call(band_kernel, out_shape=jax.ShapeDtypeStruct((CHIPS, NARROW...  2.77 us
    ppermute x1, starting transfers between devices, per_device(): other = lax.ppermute(mine, 'wide', [(i, i ^ 1) for i in range(2 * CHIPS)])  2.52 us
    ppermute x1, waiting for transfers between devices, per_device(): other = lax.ppermute(mine, 'wide', [(i, i ^ 1) for i in range(2 * CHIPS)])  2.29 us
  transfers between devices with their start and end apart: 1, of which 1 were waited for; matrix products, arithmetic and copies ran while one was open for 0% of the time, Pallas kernels for 0%

profile of v1, /device:TPU:1, one launch (start us, length us, event | category | flops | bytes accessed | tf_op | source)
XLA Modules:
  0.0 62.3 jit_solution(10634152761243413191)
XLA Ops:
  0.0 2.8 %band.1 = bf16[8,8,64,128]{3,2,1,0:T(8,128)(2,1)} custom-call(f32[3,256]{1,0:T(4,128)} %scale_v.1, f32[3,256]{1,0:T(4,128)} %scale_v.1, bf16[2,16,32,256]{3,2,1,0:T(8,128)(2,1)} %image.1, bf16[512,128]{1,0:T(8,128)(2,1)} %constant.15.z_table), custom_call_target="tpu_custom_call" | custom-call | tf_op jit(solution)/shard_map/band/pallas_call | solution.py:134
  2.8 28.3 %all_to_all.5 = bf16[64,64,128]{2,1,0:T(8,128)(2,1)S(1)} all-to-all(bf16[64,64,128]{2,1,0:T(8,128)(2,1)} %bitcast.9), channel_id=1, replica_groups={{0,1,2,3,4,5,6,7,16,17,18,19,20,21,22,23,32,33,34,35,36,37,38,39,48,49,..., dimensions={0} | all-to-all | bytes 2097152 | tf_op jit(solution)/shard_map/all_to_all | solution.py:144
  31.1 0.0 copy-start
  31.1 2.5 %collective-permute-start = (bf16[64,64,128]{2,1,0:T(8,128)(2,1)S(1)}, bf16[64,64,128]{2,1,0:T(8,128)(2,1)S(1)}, u32[]{:S(2)}, u32[]{:S(2)}) collective-permute-start(bf16[64,64,128]{2,1,0:T(8,128)(2,1)S(1)} %all_to_all.5), channel_id=1, source_target_pairs={{0,8},{8,0},{16,24},{24,16},{32,40},{40,32},{48,56},{56,48},{64,72... | collective-permute-start | bytes 3145736 | tf_op jit(solution)/shard_map/ppermute | solution.py:146
  33.6 2.3 %collective-permute-done = bf16[64,64,128]{2,1,0:T(8,128)(2,1)S(1)} collective-permute-done((bf16[64,64,128]{2,1,0:T(8,128)(2,1)S(1)}, bf16[64,64,128]{2,1,0:T(8,128)(2,1)S(1)}, u32[]{:S(2)}, u32[]{:S(2)}) %collective-permute-start) | collective-permute-done | bytes 1048608 | tf_op jit(solution)/shard_map/ppermute | solution.py:146
  35.9 0.0 copy-start.1
  35.9 0.0 copy-done
  35.9 1.0 %copy-done.1 = bf16[64,64,128]{2,1,0:T(8,128)(2,1)} copy-done((bf16[64,64,128]{2,1,0:T(8,128)(2,1)}, bf16[64,64,128]{2,1,0:T(8,128)(2,1)S(1)}, u32[]{:S(2)}) %copy-start.1) | copy-done | bytes 1048600
  36.9 25.5 %samples.1 = f32[16,2,1536]{2,1,0:T(2,128)} custom-call(s32[1,16]{1,0:T(1,128)} %offsets.1, bf16[8,512,128]{2,1,0:T(8,128)(2,1)} %bitcast.8, bf16[8,512,128]{2,1,0:T(8,128)(2,1)} %bitcast.10, bf16[1024,512]{1,0:T(8,128)(2,1)} %constant.16.y_table, bf16[512,512]{1,0:T(8,128)(2,1)} %constant.17.x_table, f32[264,512]{1,0:T(8,128)} %constant.11.clone.phase, ...), custom_call_target="tpu_custom_call" | custom-call | tf_op jit(solution)/shard_map/samples/pallas_call | solution.py:147
Async XLA Ops:
  31.1 4.8 %copy-start = (bf16[64,64,128]{2,1,0:T(8,128)(2,1)}, bf16[64,64,128]{2,1,0:T(8,128)(2,1)S(1)}, u32[]{:S(2)}) copy-start(bf16[64,64,128]{2,1,0:T(8,128)(2,1)S(1)} %all_to_all.5) | copy-start | bytes 3145732
  31.1 4.8 %collective-permute-start = (bf16[64,64,128]{2,1,0:T(8,128)(2,1)S(1)}, bf16[64,64,128]{2,1,0:T(8,128)(2,1)S(1)}, u32[]{:S(2)}, u32[]{:S(2)}) collective-permute-start(bf16[64,64,128]{2,1,0:T(8,128)(2,1)S(1)} %all_to_all.5), channel_id=1, source_target_pairs={{0,8},{8,0},{16,24},{24,16},{32,40},{40,32},{48,56},{56,48},{64,72... | collective-permute-start | bytes 3145736 | tf_op jit(solution)/shard_map/ppermute | solution.py:146
  35.9 1.0 %copy-start.1 = (bf16[64,64,128]{2,1,0:T(8,128)(2,1)}, bf16[64,64,128]{2,1,0:T(8,128)(2,1)S(1)}, u32[]{:S(2)}) copy-start(bf16[64,64,128]{2,1,0:T(8,128)(2,1)S(1)} %collective-permute-done) | copy-start | bytes 3145732

commit v2 on v1

v2 whole, which is shorter than its diff:
```python
import math

import jax
import jax.numpy as jnp
import numpy as np
from jax import lax
from jax.experimental import pallas as pl
from jax.experimental.pallas import tpu as pltpu
from jax.sharding import PartitionSpec as P

N = 256
G = 512
KZ = 64
SAMP = 1536
SLABS = 16
NARROW = 8
CHIPS = 8
XB = 16
YB = 32
ZB = KZ // NARROW


def trig(frequency, position):
    phase = np.mod(np.asarray(frequency, np.int64)[:, None] * np.asarray(position, np.int64)[None, :], G)
    angle = phase.astype(np.float32) * np.float32(2.0 * math.pi / G)
    factor = np.float32(1.0 / math.sqrt(N))
    return (np.cos(angle) * factor).astype(np.float32), (np.sin(angle) * factor).astype(np.float32)


def complex_table(cosine, sine):
    real = np.stack([cosine, sine], axis=1)
    imag = np.stack([-sine, cosine], axis=1)
    return np.stack([real, imag], axis=0)


def tables():
    position = np.arange(N) - N // 2
    z = complex_table(*trig(np.arange(KZ) - KZ // 2, position))
    z = z.reshape(2, NARROW, ZB, 2, N).transpose(3, 4, 2, 1, 0).reshape(2 * N, ZB * NARROW * 2)
    y = complex_table(*trig(np.arange(G) - G // 2, position))
    y = y.reshape(2, G, 2, NARROW, YB).transpose(0, 1, 3, 2, 4).reshape(2 * G, 2 * N)
    order = np.arange(N).reshape(CHIPS, 2, XB).transpose(1, 0, 2).reshape(N)
    x = complex_table(*trig(np.arange(N) - G // 2, position[order]))
    x = x.reshape(2 * N, 2, 2, N // 2)
    x = np.stack([x, x[:, :, ::-1]]).reshape(2, 2 * N, 2 * N)
    pc, ps = trig(np.arange(N + 8), position[order])
    phase = np.concatenate([pc, ps], axis=1) * np.float32(math.sqrt(N))
    as_bf16 = lambda t: jnp.asarray(t, jnp.float32).astype(jnp.bfloat16)
    return as_bf16(z), as_bf16(y), as_bf16(x), jnp.asarray(phase, jnp.float32)


def nt(a, b):
    return lax.dot_general(a, b, (((1,), (1,)), ((), ())), preferred_element_type=jnp.float32)


def load_all(pairs, sems):
    loads = [pltpu.make_async_copy(source, target, sems.at[i]) for i, (source, target) in enumerate(pairs)]
    for load in loads:
        load.start()
    for load in loads:
        load.wait()


def band_kernel(scale_hbm, image_hbm, z_hbm, out, scale_s, scale_v, image, z_table, rows, sems):
    wide = lax.axis_index("wide")
    narrow = lax.axis_index("narrow")
    load_all([(scale_hbm, scale_s), (scale_hbm, scale_v), (image_hbm, image), (z_hbm, z_table)], sems)
    lane = lax.broadcasted_iota(jnp.int32, (YB, N), 1)
    row = lax.broadcasted_iota(jnp.int32, (YB, N), 0)
    picked = jnp.where(lane == row + narrow * YB, scale_v[1:2, :], 0.0)
    scale_y = jnp.sum(picked, axis=1, keepdims=True)
    scale_z = scale_v[2:3, :]
    for x in range(XB):
        scale_x = scale_s[0, wide * XB + x]
        for c in range(2):
            value = image[c, x].astype(jnp.float32) * scale_x * scale_y * scale_z
            rows[x * YB:(x + 1) * YB, c * N:(c + 1) * N] = value.astype(jnp.bfloat16)
    product = jnp.dot(rows[...], z_table[...], preferred_element_type=jnp.float32)
    part = [product[x * YB:(x + 1) * YB] for x in range(XB)]
    lanes = lax.broadcasted_iota(jnp.int32, (YB, 128), 1)
    for bit in range(4):
        d = 1 << bit
        low = (lanes & d) == 0
        for i in range(XB):
            if i & d:
                continue
            a, b = part[i], part[i | d]
            part[i] = jnp.where(low, a, pltpu.roll(b, d, 1))
            part[i | d] = jnp.where(low, pltpu.roll(a, 128 - d, 1), b)
    for g in range(2 * NARROW):
        value = part[g].astype(jnp.bfloat16)
        for chip in range(CHIPS):
            out[chip, g // 2, (g % 2) * YB:(g % 2 + 1) * YB, :] = value


def table_kernel(offsets_hbm, phase_hbm, y_hbm, x_hbm, y_table, x_table, turn, offsets, phase, sems):
    core = lax.rem(lax.axis_index("wide"), 2)
    load_all([(offsets_hbm, offsets), (phase_hbm, phase), (y_hbm, y_table), (x_hbm.at[core], x_table)], sems)
    for s in range(SLABS):
        found = phase[pl.ds(offsets[0, s], 1), :]
        swapped = jnp.concatenate([found[:, 128:256], found[:, 0:128], found[:, 384:512], found[:, 256:384]], axis=1)
        turn[s:s + 1, :] = jnp.where(core == 0, found, swapped)


def transform_lines(source, y_table, turned, out):
    for chip in range(CHIPS):
        flat = source[chip].T
        for k in range(ZB):
            turned[k, chip * XB:(chip + 1) * XB, :] = flat[k * XB:(k + 1) * XB]
    for k in range(0, ZB, 2):
        lines = nt(y_table[...], turned[k:k + 2].reshape(N, 2 * N))
        for part in range(2):
            for i in range(2):
                out[part, pl.ds(k + i, G, stride=ZB), :] = lines[part * G:(part + 1) * G, i * 128:(i + 1) * 128]


def line_kernel(source, y_table, out, turned):
    transform_lines(source, y_table, turned, out)


def sample_kernel(own, other, y_table, x_table, turn, cross_hbm, gain_hbm, out,
                  rest, turned, cross, gain, even, odd, cross_sem, gain_sem):
    for s in range(SLABS):
        pltpu.make_async_copy(cross_hbm.at[s], cross.at[s], cross_sem.at[s]).start()
        pltpu.make_async_copy(gain_hbm.at[s], gain.at[s], gain_sem.at[s]).start()
    transform_lines(other, y_table, turned, rest)

    def window(s, ref):
        angle = turn[pl.ds(s, 1), :]
        start = pl.multiple_of(s * N, N)
        real_parts, imag_parts = [], []
        for half, columns in enumerate((own, rest)):
            cosine = angle[:, half * 128:(half + 1) * 128]
            sine = angle[:, N + half * 128:N + (half + 1) * 128]
            real = columns[0, pl.ds(start, N), :]
            imag = columns[1, pl.ds(start, N), :]
            real_parts.append((real * cosine + imag * sine).astype(jnp.bfloat16))
            imag_parts.append((imag * cosine - real * sine).astype(jnp.bfloat16))
        value = jnp.concatenate(real_parts + imag_parts, axis=1)
        ref[...] = nt(x_table[...], value).astype(jnp.bfloat16)

    def gather_rows(s, ref):
        for t in range(SAMP // N):
            cut = slice(t * N, (t + 1) * N)
            partial = nt(ref[...], cross[s, cut, :])
            weight = gain[s, cut, :].T.astype(jnp.float32)
            out[s, 0:1, cut] = jnp.sum(partial[:N] * weight, axis=0, keepdims=True)
            out[s, 1:2, cut] = jnp.sum(partial[N:] * weight, axis=0, keepdims=True)

    def arrive(s):
        pltpu.make_async_copy(cross_hbm.at[s], cross.at[s], cross_sem.at[s]).wait()
        pltpu.make_async_copy(gain_hbm.at[s], gain.at[s], gain_sem.at[s]).wait()

    window(0, even)

    def two_slabs(i, carry):
        s = 2 * i
        arrive(s)
        arrive(s + 1)
        gather_rows(s, even)
        window(s + 1, odd)
        gather_rows(s + 1, odd)
        window(jnp.minimum(s + 2, SLABS - 1), even)
        return carry

    lax.fori_loop(0, SLABS // 2, two_slabs, 0)


def per_device(image, deapodization, offsets, cross_weight, x_weight):
    z_table, y_table, x_table, phase = tables()
    vmem = pl.BlockSpec(memory_space=pltpu.VMEM)
    hbm = pl.BlockSpec(memory_space=pltpu.HBM)
    mib = 1024 * 1024
    band = pl.pallas_call(
        band_kernel,
        out_shape=jax.ShapeDtypeStruct((CHIPS, NARROW, 2 * YB, 128), jnp.bfloat16),
        in_specs=[hbm] * 3,
        out_specs=vmem,
        scratch_shapes=[
            pltpu.SMEM((3, N), jnp.float32),
            pltpu.VMEM((3, N), jnp.float32),
            pltpu.VMEM((2, XB, YB, N), jnp.bfloat16),
            pltpu.VMEM((2 * N, 128), jnp.bfloat16),
            pltpu.VMEM((XB * YB, 2 * N), jnp.bfloat16),
            pltpu.SemaphoreType.DMA((4,)),
        ],
        compiler_params=pltpu.CompilerParams(vmem_limit_bytes=61 * mib),
        name="band",
    )(deapodization, image, z_table)
    y_table, x_table, turn = pl.pallas_call(
        table_kernel,
        out_shape=[
            jax.ShapeDtypeStruct((2 * G, 2 * N), jnp.bfloat16),
            jax.ShapeDtypeStruct((2 * N, 2 * N), jnp.bfloat16),
            jax.ShapeDtypeStruct((SLABS, 2 * N), jnp.float32),
        ],
        in_specs=[hbm] * 4,
        out_specs=[vmem] * 3,
        scratch_shapes=[
            pltpu.SMEM((1, SLABS), jnp.int32),
            pltpu.VMEM((N + 8, 2 * N), jnp.float32),
            pltpu.SemaphoreType.DMA((4,)),
        ],
        compiler_params=pltpu.CompilerParams(vmem_limit_bytes=8 * mib),
        name="tables",
    )(offsets, phase, y_table, x_table)
    groups = [[(chip * 2 + core) * NARROW + n for chip in range(CHIPS) for n in range(NARROW)]
              for core in range(2)]
    mine = lax.all_to_all(band.reshape(CHIPS * NARROW, 2 * YB, 128), ("wide", "narrow"), 0, 0,
                          axis_index_groups=groups, tiled=True)
    mine, y_table, x_table, turn = lax.optimization_barrier((mine, y_table, x_table, turn))
    other = lax.ppermute(mine, "wide", [(i, i ^ 1) for i in range(2 * CHIPS)])
    blocks = (CHIPS, NARROW * 2 * YB, 128)
    own = pl.pallas_call(
        line_kernel,
        out_shape=jax.ShapeDtypeStruct((2, G * ZB, 128), jnp.float32),
        in_specs=[vmem, vmem],
        out_specs=vmem,
        scratch_shapes=[pltpu.VMEM((ZB, 128, 2 * N), jnp.bfloat16)],
        compiler_params=pltpu.CompilerParams(vmem_limit_bytes=16 * mib),
        cost_estimate=pl.CostEstimate(flops=2 ** 30, bytes_accessed=6 * mib, transcendentals=0),
        name="lines",
    )(mine.reshape(blocks), y_table)
    result = pl.pallas_call(
        sample_kernel,
        out_shape=jax.ShapeDtypeStruct((SLABS, 2, SAMP), jnp.float32),
        in_specs=[vmem] * 5 + [hbm] * 2,
        out_specs=vmem,
        scratch_shapes=[
            pltpu.VMEM((2, G * ZB, 128), jnp.float32),
            pltpu.VMEM((ZB, 128, 2 * N), jnp.bfloat16),
            pltpu.VMEM((SLABS, SAMP, N), jnp.bfloat16),
            pltpu.VMEM((SLABS, SAMP, N), jnp.bfloat16),
            pltpu.VMEM((2 * N, N), jnp.bfloat16),
            pltpu.VMEM((2 * N, N), jnp.bfloat16),
            pltpu.SemaphoreType.DMA((SLABS,)),
            pltpu.SemaphoreType.DMA((SLABS,)),
        ],
        compiler_params=pltpu.CompilerParams(vmem_limit_bytes=44 * mib),
        name="samples",
    )(own, other.reshape(blocks), y_table, x_table, turn, cross_weight[0], x_weight[0])
    return result[None]


def solution(mesh):
    return jax.shard_map(
        per_device,
        mesh=mesh,
        in_specs=(
            P(None, "wide", "narrow", None),
            P(),
            P(("wide", "narrow"), None),
            P(("wide", "narrow"), None, None, None),
            P(("wide", "narrow"), None, None, None),
        ),
        out_specs=P(("wide", "narrow"), None, None, None),
        check_vma=False,
    )
```

time: 62.6 us -> 50.3 us (0.80)
  blocking collectives: 28.3 us -> 0 us
  starting transfers between devices: 2.52 us -> 14.5 us
  waiting for transfers between devices: 2.29 us -> 12.2 us
  Pallas kernels: 28.2 us -> 19.1 us
  local copies, waits for them, and re-layouts: 1.02 us -> 4.15 us
    all_to_all x1 -> x0, blocking collectives: 28.3 us -> none  [per_device(): lax.all_to_all(band.reshape(CHIPS * NARROW, 2 * YB, 128), ('wide', 'narro...]
    all_to_all x0 -> x1, starting transfers between devices: none -> 12 us  [per_device(): lax.all_to_all(band.reshape(CHIPS * NARROW, 2 * YB, 128), ('wide', 'narro...]
    all_to_all x0 -> x1, waiting for transfers between devices: none -> 11.6 us  [per_device(): lax.all_to_all(band.reshape(CHIPS * NARROW, 2 * YB, 128), ('wide', 'narro...]
    pallas_call x1, Pallas kernels: 25.5 us -> 14.1 us  [per_device(): pl.pallas_call(sample_kernel, out_shape=jax.ShapeDtypeStruct((SLABS, 2, S...]
    unnamed x4 -> x8, local copies, waits for them, and re-layouts: 1.02 us -> 4.15 us
    pallas_call x0 -> x2, Pallas kernels: none -> 2.21 us  [the longest x1 1.6 us: per_device(): pl.pallas_call(line_kernel, out_shape=jax.ShapeDtypeStruct((2, G * ZB, 12...]
    ppermute x1, waiting for transfers between devices: 2.29 us -> 0.68 us  [per_device(): other = lax.ppermute(mine, 'wide', [(i, i ^ 1) for i in range(2 * CHIPS)])]
  transfers between devices with their start and end apart: 1 -> 2, of which waited for: 1 -> 2; matrix products, arithmetic and copies ran while one was open for 0% -> 0% of each run, Pallas kernels for 0% -> 4%
where the time goes in v2:
time: 50.3 us; the launch traced here: 50 us
  Pallas kernels  19.1 us (38%)
  starting transfers between devices  14.5 us (29%)
  waiting for transfers between devices  12.2 us (24%)
  local copies, waits for them, and re-layouts  4.15 us (8%)
    pallas_call x1, Pallas kernels, per_device(): pl.pallas_call(sample_kernel, out_shape=jax.ShapeDtypeStruct((SLABS, 2, S...  14.1 us
    all_to_all x1, starting transfers between devices, per_device(): lax.all_to_all(band.reshape(CHIPS * NARROW, 2 * YB, 128), ('wide', 'narro...  12 us
    all_to_all x1, waiting for transfers between devices, per_device(): lax.all_to_all(band.reshape(CHIPS * NARROW, 2 * YB, 128), ('wide', 'narro...  11.6 us
    unnamed x8, local copies, waits for them, and re-layouts  4.15 us
    pallas_call x1, Pallas kernels, per_device(): pl.pallas_call(band_kernel, out_shape=jax.ShapeDtypeStruct((CHIPS, NARROW...  2.79 us
    ppermute x1, starting transfers between devices, per_device(): other = lax.ppermute(mine, 'wide', [(i, i ^ 1) for i in range(2 * CHIPS)])  2.52 us
    pallas_call x1, Pallas kernels, per_device(): pl.pallas_call(line_kernel, out_shape=jax.ShapeDtypeStruct((2, G * ZB, 12...  1.6 us
  transfers between devices with their start and end apart: 2, of which 2 were waited for; matrix products, arithmetic and copies ran while one was open for 0% of the time, Pallas kernels for 4%

profile of v2, /device:TPU:1, one launch (start us, length us, event | category | flops | bytes accessed | tf_op | source)
XLA Modules:
  0.0 50.0 jit_solution(17621360416249944595)
XLA Ops:
  0.0 2.8 %band.1 = bf16[8,8,64,128]{3,2,1,0:T(8,128)(2,1)} custom-call(f32[3,256]{1,0:T(4,128)} %scale_hbm.1, bf16[2,16,32,256]{3,2,1,0:T(8,128)(2,1)} %image_hbm.1, bf16[512,128]{1,0:T(8,128)(2,1)} %constant.15.z_hbm), custom_call_target="tpu_custom_call" | custom-call | tf_op jit(solution)/shard_map/band/pallas_call | solution.py:174
  2.8 12.0 %all-to-all-start = ((bf16[64,64,128]{2,1,0:T(8,128)(2,1)}), bf16[64,64,128]{2,1,0:T(8,128)(2,1)S(1)}, u32[]{:S(2)}, u32[]{:S(2)}) async-start(bf16[64,64,128]{2,1,0:T(8,128)(2,1)} %bitcast.10), calls=%async_computation | async-start | bytes 2097152 | tf_op jit(solution)/shard_map/all_to_all | solution.py:209
  14.8 0.0 copy-start
  14.8 1.2 %copy-done = bf16[2,512,512]{2,1,0:T(8,128)(2,1)S(1)} copy-done((bf16[2,512,512]{2,1,0:T(8,128)(2,1)S(1)}, bf16[2,512,512]{2,1,0:T(8,128)(2,1)}, u32[]{:S(2)}) %copy-start) | copy-done | bytes 1048600
  16.0 0.0 copy-start.1
  16.0 1.2 %copy-done.1 = bf16[1024,512]{1,0:T(8,128)(2,1)S(1)} copy-done((bf16[1024,512]{1,0:T(8,128)(2,1)S(1)}, bf16[1024,512]{1,0:T(8,128)(2,1)}, u32[]{:S(2)}) %copy-start.1) | copy-done | bytes 1048600
  17.2 0.0 copy-start.2
  17.2 1.0 %copy-done.2 = f32[264,512]{1,0:T(8,128)S(1)} copy-done((f32[264,512]{1,0:T(8,128)S(1)}, f32[264,512]{1,0:T(8,128)}, u32[]{:S(2)}) %copy-start.2) | copy-done | bytes 540696
  18.3 0.0 copy-start.3
  18.3 0.7 %copy-done.3 = s32[1,16]{1,0:T(1,128)S(1)} copy-done((s32[1,16]{1,0:T(1,128)S(1)}, s32[1,16]{1,0:T(1,128)}, u32[]{:S(2)}) %copy-start.3) | copy-done | bytes 88
  18.9 0.6 %tables.1 = (bf16[1024,512]{1,0:T(8,128)(2,1)S(1)}, bf16[512,512]{1,0:T(8,128)(2,1)S(1)}, f32[16,512]{1,0:T(8,128)S(1)}) custom-call(s32[1,16]{1,0:T(1,128)S(1)} %copy-done.3, f32[264,512]{1,0:T(8,128)S(1)} %copy-done.2, bf16[1024,512]{1,0:T(8,128)(2,1)S(1)} %copy-done.1, bf16[2,512,512]{2,1,0:T(8,128)(2,1)S(1)} %copy-done), custom_call_target="tpu_custom_call" | custom-call | tf_op jit(solution)/shard_map/tables/pallas_call | solution.py:190
  19.5 11.6 %all-to-all-done = bf16[64,64,128]{2,1,0:T(8,128)(2,1)S(1)} async-done(((bf16[64,64,128]{2,1,0:T(8,128)(2,1)}), bf16[64,64,128]{2,1,0:T(8,128)(2,1)S(1)}, u32[]{:S(2)}, u32[]{:S(2)}) %all-to-all-start) | async-done | bytes 1048608 | tf_op jit(solution)/shard_map/all_to_all | solution.py:209
  31.1 2.5 %collective-permute-start = (bf16[64,64,128]{2,1,0:T(8,128)(2,1)S(1)}, bf16[64,64,128]{2,1,0:T(8,128)(2,1)S(1)}, u32[]{:S(2)}, u32[]{:S(2)}) collective-permute-start(bf16[64,64,128]{2,1,0:T(8,128)(2,1)S(1)} %all-to-all-done), channel_id=1, source_target_pairs={{0,8},{8,0},{16,24},{24,16},{32,40},{40,32},{48,56},{56,48},{64,72... | collective-permute-start | bytes 3145736 | tf_op jit(solution)/shard_map/ppermute | solution.py:212
  33.6 1.6 %lines.1.own = f32[2,4096,128]{2,1,0:T(8,128)S(1)} custom-call(bf16[8,512,128]{2,1,0:T(8,128)(2,1)S(1)} %bitcast.6, bf16[1024,512]{1,0:T(8,128)(2,1)S(1)} %get-tuple-element.16.y_table), custom_call_target="tpu_custom_call" | custom-call | flops 1073741824 | bytes 6291456 | tf_op jit(solution)/shard_map/lines/pallas_call | solution.py:214
  35.2 0.7 %collective-permute-done = bf16[64,64,128]{2,1,0:T(8,128)(2,1)S(1)} collective-permute-done((bf16[64,64,128]{2,1,0:T(8,128)(2,1)S(1)}, bf16[64,64,128]{2,1,0:T(8,128)(2,1)S(1)}, u32[]{:S(2)}, u32[]{:S(2)}) %collective-permute-start) | collective-permute-done | bytes 1048608 | tf_op jit(solution)/shard_map/ppermute | solution.py:212
  35.9 14.1 %samples.1 = f32[16,2,1536]{2,1,0:T(2,128)} custom-call(f32[2,4096,128]{2,1,0:T(8,128)S(1)} %lines.1.own, bf16[8,512,128]{2,1,0:T(8,128)(2,1)S(1)} %bitcast.7, bf16[1024,512]{1,0:T(8,128)(2,1)S(1)} %get-tuple-element.16.y_table, bf16[512,512]{1,0:T(8,128)(2,1)S(1)} %get-tuple-element.17.x_table, f32[16,512]{1,0:T(8,128)S(1)} %get-tuple-element.18.turn, ...), custom_call_target="tpu_custom_call" | custom-call | tf_op jit(solution)/shard_map/samples/pallas_call | solution.py:224
Async XLA Ops:
  2.8 28.3 %all-to-all-start = ((bf16[64,64,128]{2,1,0:T(8,128)(2,1)}), bf16[64,64,128]{2,1,0:T(8,128)(2,1)S(1)}, u32[]{:S(2)}, u32[]{:S(2)}) async-start(bf16[64,64,128]{2,1,0:T(8,128)(2,1)} %bitcast.10), calls=%async_computation | async-start | bytes 2097152 | tf_op jit(solution)/shard_map/all_to_all | solution.py:209
  14.8 1.2 %copy-start = (bf16[2,512,512]{2,1,0:T(8,128)(2,1)S(1)}, bf16[2,512,512]{2,1,0:T(8,128)(2,1)}, u32[]{:S(2)}) copy-start(bf16[2,512,512]{2,1,0:T(8,128)(2,1)} %constant.17.x_hbm) | copy-start | bytes 3145732
  16.0 1.2 %copy-start.1 = (bf16[1024,512]{1,0:T(8,128)(2,1)S(1)}, bf16[1024,512]{1,0:T(8,128)(2,1)}, u32[]{:S(2)}) copy-start(bf16[1024,512]{1,0:T(8,128)(2,1)} %constant.16.y_hbm) | copy-start | bytes 3145732
  17.2 1.0 %copy-start.2 = (f32[264,512]{1,0:T(8,128)S(1)}, f32[264,512]{1,0:T(8,128)}, u32[]{:S(2)}) copy-start(f32[264,512]{1,0:T(8,128)} %constant.11.clone.phase_hbm) | copy-start | bytes 1622020
  18.3 0.7 %copy-start.3 = (s32[1,16]{1,0:T(1,128)S(1)}, s32[1,16]{1,0:T(1,128)}, u32[]{:S(2)}) copy-start(s32[1,16]{1,0:T(1,128)} %offsets_hbm.1) | copy-start | bytes 196
  31.1 4.8 %collective-permute-start = (bf16[64,64,128]{2,1,0:T(8,128)(2,1)S(1)}, bf16[64,64,128]{2,1,0:T(8,128)(2,1)S(1)}, u32[]{:S(2)}, u32[]{:S(2)}) collective-permute-start(bf16[64,64,128]{2,1,0:T(8,128)(2,1)S(1)} %all-to-all-done), channel_id=1, source_target_pairs={{0,8},{8,0},{16,24},{24,16},{32,40},{40,32},{48,56},{56,48},{64,72... | collective-permute-start | bytes 3145736 | tf_op jit(solution)/shard_map/ppermute | solution.py:212

commit v3 on v2

--- a/solution.py
+++ b/solution.py
@@ -13,6 +13,7 @@
 KZ = 64
 SAMP = 1536
 SLABS = 16
+STEP = 4
 NARROW = 8
 CHIPS = 8
 XB = 16
@@ -41,12 +42,25 @@
     y = y.reshape(2, G, 2, NARROW, YB).transpose(0, 1, 3, 2, 4).reshape(2 * G, 2 * N)
     order = np.arange(N).reshape(CHIPS, 2, XB).transpose(1, 0, 2).reshape(N)
     x = complex_table(*trig(np.arange(N) - G // 2, position[order]))
-    x = x.reshape(2 * N, 2, 2, N // 2)
-    x = np.stack([x, x[:, :, ::-1]]).reshape(2, 2 * N, 2 * N)
+    x = x.reshape(2 * N, 2 * N)
     pc, ps = trig(np.arange(N + 8), position[order])
     phase = np.concatenate([pc, ps], axis=1) * np.float32(math.sqrt(N))
     as_bf16 = lambda t: jnp.asarray(t, jnp.float32).astype(jnp.bfloat16)
     return as_bf16(z), as_bf16(y), as_bf16(x), jnp.asarray(phase, jnp.float32)
+
+
+def exchange_order():
+    spots = [(x, y, z) for x in range(4) for y in range(4) for z in range(4)][::-1]
+    spots = spots[16:] + spots[:16]
+    return [(x // 2 * 4 + y, z * 2 + x % 2) for x, y, z in spots]
+
+
+SPOTS = exchange_order()
+WHERE = {spot: i for i, spot in enumerate(SPOTS)}
+
+
+def in_hbm(*arrays):
+    return [pltpu.with_memory_space_constraint(array, pltpu.HBM) for array in arrays]
 
 
 def nt(a, b):
@@ -90,21 +104,26 @@
     for g in range(2 * NARROW):
         value = part[g].astype(jnp.bfloat16)
         for chip in range(CHIPS):
-            out[chip, g // 2, (g % 2) * YB:(g % 2 + 1) * YB, :] = value
-
-
-def table_kernel(offsets_hbm, phase_hbm, y_hbm, x_hbm, y_table, x_table, turn, offsets, phase, sems):
+            out[WHERE[chip, g // 2], (g % 2) * YB:(g % 2 + 1) * YB, :] = value
+
+
+def table_kernel(offsets_hbm, phase_hbm, y_hbm, x_hbm, y_table, x_table, turn, offsets, phase, x_any, sems):
     core = lax.rem(lax.axis_index("wide"), 2)
-    load_all([(offsets_hbm, offsets), (phase_hbm, phase), (y_hbm, y_table), (x_hbm.at[core], x_table)], sems)
+    load_all([(offsets_hbm, offsets), (phase_hbm, phase), (y_hbm, y_table), (x_hbm, x_any)], sems)
+
+    def ordered(found):
+        swapped = jnp.concatenate([found[:, 128:256], found[:, 0:128], found[:, 384:512], found[:, 256:384]], axis=1)
+        return jnp.where(core == 0, found, swapped)
+
+    x_table[...] = ordered(x_any[...])
     for s in range(SLABS):
         found = phase[pl.ds(offsets[0, s], 1), :]
-        swapped = jnp.concatenate([found[:, 128:256], found[:, 0:128], found[:, 384:512], found[:, 256:384]], axis=1)
-        turn[s:s + 1, :] = jnp.where(core == 0, found, swapped)
+        turn[s:s + 1, :] = ordered(found)
 
 
 def transform_lines(source, y_table, turned, out):
     for chip in range(CHIPS):
-        flat = source[chip].T
+        flat = jnp.concatenate([source[WHERE[chip, n]] for n in range(NARROW)], axis=0).T
         for k in range(ZB):
             turned[k, chip * XB:(chip + 1) * XB, :] = flat[k * XB:(k + 1) * XB]
     for k in range(0, ZB, 2):
@@ -120,10 +139,14 @@
 
 def sample_kernel(own, other, y_table, x_table, turn, cross_hbm, gain_hbm, out,
                   rest, turned, cross, gain, even, odd, cross_sem, gain_sem):
-    for s in range(SLABS):
-        pltpu.make_async_copy(cross_hbm.at[s], cross.at[s], cross_sem.at[s]).start()
-        pltpu.make_async_copy(gain_hbm.at[s], gain.at[s], gain_sem.at[s]).start()
+    def fetch(first, last):
+        for s in range(first, last):
+            pltpu.make_async_copy(cross_hbm.at[s], cross.at[s], cross_sem.at[s]).start()
+            pltpu.make_async_copy(gain_hbm.at[s], gain.at[s], gain_sem.at[s]).start()
+
+    fetch(0, 4)
     transform_lines(other, y_table, turned, rest)
+    fetch(4, 16)
 
     def window(s, ref):
         angle = turn[pl.ds(s, 1), :]
@@ -147,23 +170,27 @@
             out[s, 0:1, cut] = jnp.sum(partial[:N] * weight, axis=0, keepdims=True)
             out[s, 1:2, cut] = jnp.sum(partial[N:] * weight, axis=0, keepdims=True)
 
-    def arrive(s):
-        pltpu.make_async_copy(cross_hbm.at[s], cross.at[s], cross_sem.at[s]).wait()
-        pltpu.make_async_copy(gain_hbm.at[s], gain.at[s], gain_sem.at[s]).wait()
+    def some_slabs(first, count):
+        for j in range(count):
+            s = first + j
+            pltpu.make_async_copy(cross_hbm.at[s], cross.at[s], cross_sem.at[s]).wait()
+            pltpu.make_async_copy(gain_hbm.at[s], gain.at[s], gain_sem.at[s]).wait()
+        for j in range(0, count, 2):
+            s = first + j
+            gather_rows(s, even)
+            window(s + 1, odd)
+            gather_rows(s + 1, odd)
+            window(jnp.minimum(s + 2, SLABS - 1), even)
 
     window(0, even)
-
-    def two_slabs(i, carry):
-        s = 2 * i
-        arrive(s)
-        arrive(s + 1)
-        gather_rows(s, even)
-        window(s + 1, odd)
-        gather_rows(s + 1, odd)
-        window(jnp.minimum(s + 2, SLABS - 1), even)
+    some_slabs(0, 2)
+    some_slabs(2, 2)
+
+    def slabs(i, carry):
+        some_slabs(STEP * (i + 1), STEP)
         return carry
 
-    lax.fori_loop(0, SLABS // 2, two_slabs, 0)
+    lax.fori_loop(0, SLABS // STEP - 1, slabs, 0)
 
 
 def per_device(image, deapodization, offsets, cross_weight, x_weight):
@@ -173,7 +200,7 @@
     mib = 1024 * 1024
     band = pl.pallas_call(
         band_kernel,
-        out_shape=jax.ShapeDtypeStruct((CHIPS, NARROW, 2 * YB, 128), jnp.bfloat16),
+        out_shape=jax.ShapeDtypeStruct((len(SPOTS), 2 * YB, 128), jnp.bfloat16),
         in_specs=[hbm] * 3,
         out_specs=vmem,
         scratch_shapes=[
@@ -186,7 +213,7 @@
         ],
         compiler_params=pltpu.CompilerParams(vmem_limit_bytes=61 * mib),
         name="band",
-    )(deapodization, image, z_table)
+    )(*in_hbm(deapodization, image, z_table))
     y_table, x_table, turn = pl.pallas_call(
         table_kernel,
         out_shape=[
@@ -199,18 +226,16 @@
         scratch_shapes=[
             pltpu.SMEM((1, SLABS), jnp.int32),
             pltpu.VMEM((N + 8, 2 * N), jnp.float32),
+            pltpu.VMEM((2 * N, 2 * N), jnp.bfloat16),
             pltpu.SemaphoreType.DMA((4,)),
         ],
         compiler_params=pltpu.CompilerParams(vmem_limit_bytes=8 * mib),
         name="tables",
-    )(offsets, phase, y_table, x_table)
-    groups = [[(chip * 2 + core) * NARROW + n for chip in range(CHIPS) for n in range(NARROW)]
-              for core in range(2)]
-    mine = lax.all_to_all(band.reshape(CHIPS * NARROW, 2 * YB, 128), ("wide", "narrow"), 0, 0,
-                          axis_index_groups=groups, tiled=True)
+    )(*in_hbm(offsets, phase, y_table, x_table))
+    groups = [[(chip * 2 + core) * NARROW + n for chip, n in SPOTS] for core in range(2)]
+    mine = lax.all_to_all(band, ("wide", "narrow"), 0, 0, axis_index_groups=groups, tiled=True)
     mine, y_table, x_table, turn = lax.optimization_barrier((mine, y_table, x_table, turn))
     other = lax.ppermute(mine, "wide", [(i, i ^ 1) for i in range(2 * CHIPS)])
-    blocks = (CHIPS, NARROW * 2 * YB, 128)
     own = pl.pallas_call(
         line_kernel,
         out_shape=jax.ShapeDtypeStruct((2, G * ZB, 128), jnp.float32),
@@ -220,7 +245,7 @@
         compiler_params=pltpu.CompilerParams(vmem_limit_bytes=16 * mib),
         cost_estimate=pl.CostEstimate(flops=2 ** 30, bytes_accessed=6 * mib, transcendentals=0),
         name="lines",
-    )(mine.reshape(blocks), y_table)
+    )(mine, y_table)
     result = pl.pallas_call(
         sample_kernel,
         out_shape=jax.ShapeDtypeStruct((SLABS, 2, SAMP), jnp.float32),
@@ -238,7 +263,7 @@
         ],
         compiler_params=pltpu.CompilerParams(vmem_limit_bytes=44 * mib),
         name="samples",
-    )(own, other.reshape(blocks), y_table, x_table, turn, cross_weight[0], x_weight[0])
+    )(own, other, y_table, x_table, turn, *in_hbm(cross_weight[0], x_weight[0]))
     return result[None]
 
 

time: 50.3 us -> 46.6 us (0.926)
  local copies, waits for them, and re-layouts: 4.15 us -> 0 us
  starting transfers between devices: 14.5 us -> 15.2 us
    unnamed x8 -> x0, local copies, waits for them, and re-layouts: 4.15 us -> none
    all_to_all x1, starting transfers between devices: 12 us -> 13.9 us  [per_device(): lax.all_to_all(band, ('wide', 'narrow'), 0, 0, axis_index_groups=groups,...]
    ppermute x1, starting transfers between devices: 2.52 us -> 1.35 us  [per_device(): other = lax.ppermute(mine, 'wide', [(i, i ^ 1) for i in range(2 * CHIPS)])]
    pallas_call x1, Pallas kernels: 0.62 us -> 1.66 us  [per_device(): pl.pallas_call(table_kernel, out_shape=[jax.ShapeDtypeStruct((2 * G, 2 *...]
    pallas_call x1, Pallas kernels: 14.1 us -> 13.4 us  [per_device(): pl.pallas_call(sample_kernel, out_shape=jax.ShapeDtypeStruct((SLABS, 2, S...]
    all_to_all x1, waiting for transfers between devices: 11.6 us -> 11 us  [per_device(): lax.all_to_all(band, ('wide', 'narrow'), 0, 0, axis_index_groups=groups,...]
  transfers between devices with their start and end apart: 2 -> 2, of which waited for: 2 -> 2; matrix products, arithmetic and copies ran while one was open for 0% -> 0% of each run, Pallas kernels for 4% -> 7%
where the time goes in v3:
time: 46.6 us; the launch traced here: 46.4 us
  Pallas kernels  19.4 us (42%)
  starting transfers between devices  15.2 us (33%)
  waiting for transfers between devices  11.7 us (25%)
    all_to_all x1, starting transfers between devices, per_device(): lax.all_to_all(band, ('wide', 'narrow'), 0, 0, axis_index_groups=groups,...  13.9 us
    pallas_call x1, Pallas kernels, per_device(): pl.pallas_call(sample_kernel, out_shape=jax.ShapeDtypeStruct((SLABS, 2, S...  13.4 us
    all_to_all x1, waiting for transfers between devices, per_device(): lax.all_to_all(band, ('wide', 'narrow'), 0, 0, axis_index_groups=groups,...  11 us
    pallas_call x1, Pallas kernels, per_device(): pl.pallas_call(band_kernel, out_shape=jax.ShapeDtypeStruct((len(SPOTS), 2...  2.79 us
    pallas_call x1, Pallas kernels, per_device(): pl.pallas_call(table_kernel, out_shape=[jax.ShapeDtypeStruct((2 * G, 2 *...  1.66 us
    pallas_call x1, Pallas kernels, per_device(): pl.pallas_call(line_kernel, out_shape=jax.ShapeDtypeStruct((2, G * ZB, 12...  1.6 us
    ppermute x1, starting transfers between devices, per_device(): other = lax.ppermute(mine, 'wide', [(i, i ^ 1) for i in range(2 * CHIPS)])  1.35 us
  transfers between devices with their start and end apart: 2, of which 2 were waited for; matrix products, arithmetic and copies ran while one was open for 0% of the time, Pallas kernels for 7%

profile of v3, /device:TPU:1, one launch (start us, length us, event | category | flops | bytes accessed | tf_op | source)
XLA Modules:
  0.0 46.4 jit_solution(15651018866872198648)
XLA Ops:
  0.0 2.8 %band.1 = bf16[64,64,128]{2,1,0:T(8,128)(2,1)} custom-call(f32[3,256]{1,0:T(4,128)} %scale_hbm.1, bf16[2,16,32,256]{3,2,1,0:T(8,128)(2,1)} %image_hbm.1, bf16[512,128]{1,0:T(8,128)(2,1)} %constant.15.z_hbm), custom_call_target="tpu_custom_call" | custom-call | tf_op jit(solution)/shard_map/band/pallas_call | solution.py:201
  2.8 13.9 %all-to-all-start = ((bf16[64,64,128]{2,1,0:T(8,128)(2,1)}), bf16[64,64,128]{2,1,0:T(8,128)(2,1)S(1)}, u32[]{:S(2)}, u32[]{:S(2)}) async-start(bf16[64,64,128]{2,1,0:T(8,128)(2,1)} %band.1), calls=%async_computation | async-start | bytes 2097152 | tf_op jit(solution)/shard_map/all_to_all | solution.py:236
  16.7 1.7 %tables.1 = (bf16[1024,512]{1,0:T(8,128)(2,1)S(1)}, bf16[512,512]{1,0:T(8,128)(2,1)S(1)}, f32[16,512]{1,0:T(8,128)S(1)}) custom-call(s32[1,16]{1,0:T(1,128)} %offsets_hbm.1, f32[264,512]{1,0:T(8,128)} %constant.11.clone.phase_hbm, bf16[1024,512]{1,0:T(8,128)(2,1)} %constant.16.y_hbm, bf16[512,512]{1,0:T(8,128)(2,1)} %constant.17.x_hbm), custom_call_target="tpu_custom_call" | custom-call | tf_op jit(solution)/shard_map/tables/pallas_call | solution.py:217
  18.4 11.0 %all-to-all-done.source = bf16[64,64,128]{2,1,0:T(8,128)(2,1)S(1)} async-done(((bf16[64,64,128]{2,1,0:T(8,128)(2,1)}), bf16[64,64,128]{2,1,0:T(8,128)(2,1)S(1)}, u32[]{:S(2)}, u32[]{:S(2)}) %all-to-all-start) | async-done | bytes 1048608 | tf_op jit(solution)/shard_map/all_to_all | solution.py:236
  29.3 1.3 %collective-permute-start = (bf16[64,64,128]{2,1,0:T(8,128)(2,1)S(1)}, bf16[64,64,128]{2,1,0:T(8,128)(2,1)S(1)}, u32[]{:S(2)}, u32[]{:S(2)}) collective-permute-start(bf16[64,64,128]{2,1,0:T(8,128)(2,1)S(1)} %all-to-all-done.source), channel_id=1, source_target_pairs={{0,8},{8,0},{16,24},{24,16},{32,40},{40,32},{48,56},{56,48},{64,72... | collective-permute-start | bytes 3145736 | tf_op jit(solution)/shard_map/ppermute | solution.py:238
  30.7 1.6 %lines.1.own = f32[2,4096,128]{2,1,0:T(8,128)S(1)} custom-call(bf16[64,64,128]{2,1,0:T(8,128)(2,1)S(1)} %all-to-all-done.source, bf16[1024,512]{1,0:T(8,128)(2,1)S(1)} %get-tuple-element.16.y_table), custom_call_target="tpu_custom_call" | custom-call | flops 1073741824 | bytes 6291456 | tf_op jit(solution)/shard_map/lines/pallas_call | solution.py:239
  32.3 0.7 %collective-permute-done.other = bf16[64,64,128]{2,1,0:T(8,128)(2,1)S(1)} collective-permute-done((bf16[64,64,128]{2,1,0:T(8,128)(2,1)S(1)}, bf16[64,64,128]{2,1,0:T(8,128)(2,1)S(1)}, u32[]{:S(2)}, u32[]{:S(2)}) %collective-permute-start) | collective-permute-done | bytes 1048608 | tf_op jit(solution)/shard_map/ppermute | solution.py:238
  33.0 13.4 %samples.1 = f32[16,2,1536]{2,1,0:T(2,128)} custom-call(f32[2,4096,128]{2,1,0:T(8,128)S(1)} %lines.1.own, bf16[64,64,128]{2,1,0:T(8,128)(2,1)S(1)} %collective-permute-done.other, bf16[1024,512]{1,0:T(8,128)(2,1)S(1)} %get-tuple-element.16.y_table, bf16[512,512]{1,0:T(8,128)(2,1)S(1)} %get-tuple-element.17.x_table, f32[16,512]{1,0:T(8,128)S(1)} %get-tuple-element.18.turn, ...), custom_call_target="tpu_custom_call" | custom-call | tf_op jit(solution)/shard_map/samples/pallas_call | solution.py:249
Async XLA Ops:
  2.8 26.6 %all-to-all-start = ((bf16[64,64,128]{2,1,0:T(8,128)(2,1)}), bf16[64,64,128]{2,1,0:T(8,128)(2,1)S(1)}, u32[]{:S(2)}, u32[]{:S(2)}) async-start(bf16[64,64,128]{2,1,0:T(8,128)(2,1)} %band.1), calls=%async_computation | async-start | bytes 2097152 | tf_op jit(solution)/shard_map/all_to_all | solution.py:236
  29.3 3.6 %collective-permute-start = (bf16[64,64,128]{2,1,0:T(8,128)(2,1)S(1)}, bf16[64,64,128]{2,1,0:T(8,128)(2,1)S(1)}, u32[]{:S(2)}, u32[]{:S(2)}) collective-permute-start(bf16[64,64,128]{2,1,0:T(8,128)(2,1)S(1)} %all-to-all-done.source), channel_id=1, source_target_pairs={{0,8},{8,0},{16,24},{24,16},{32,40},{40,32},{48,56},{56,48},{64,72... | collective-permute-start | bytes 3145736 | tf_op jit(solution)/shard_map/ppermute | solution.py:238

commit v4 on v3

--- a/solution.py
+++ b/solution.py
@@ -49,13 +49,7 @@
     return as_bf16(z), as_bf16(y), as_bf16(x), jnp.asarray(phase, jnp.float32)
 
 
-def exchange_order():
-    spots = [(x, y, z) for x in range(4) for y in range(4) for z in range(4)][::-1]
-    spots = spots[16:] + spots[:16]
-    return [(x // 2 * 4 + y, z * 2 + x % 2) for x, y, z in spots]
-
-
-SPOTS = exchange_order()
+SPOTS = [(chip, n) for chip in range(CHIPS)[::-1] for n in range(NARROW)[::-1]]
 WHERE = {spot: i for i, spot in enumerate(SPOTS)}
 
 
@@ -103,8 +97,7 @@
             part[i | d] = jnp.where(low, pltpu.roll(a, 128 - d, 1), b)
     for g in range(2 * NARROW):
         value = part[g].astype(jnp.bfloat16)
-        for chip in range(CHIPS):
-            out[WHERE[chip, g // 2], (g % 2) * YB:(g % 2 + 1) * YB, :] = value
+        out[NARROW - 1 - g // 2, (g % 2) * YB:(g % 2 + 1) * YB, :] = value
 
 
 def table_kernel(offsets_hbm, phase_hbm, y_hbm, x_hbm, y_table, x_table, turn, offsets, phase, x_any, sems):
@@ -200,7 +193,7 @@
     mib = 1024 * 1024
     band = pl.pallas_call(
         band_kernel,
-        out_shape=jax.ShapeDtypeStruct((len(SPOTS), 2 * YB, 128), jnp.bfloat16),
+        out_shape=jax.ShapeDtypeStruct((NARROW, 2 * YB, 128), jnp.bfloat16),
         in_specs=[hbm] * 3,
         out_specs=vmem,
         scratch_shapes=[
@@ -211,7 +204,7 @@
             pltpu.VMEM((XB * YB, 2 * N), jnp.bfloat16),
             pltpu.SemaphoreType.DMA((4,)),
         ],
-        compiler_params=pltpu.CompilerParams(vmem_limit_bytes=61 * mib),
+        compiler_params=pltpu.CompilerParams(vmem_limit_bytes=16 * mib),
         name="band",
     )(*in_hbm(deapodization, image, z_table))
     y_table, x_table, turn = pl.pallas_call(
@@ -233,6 +226,7 @@
         name="tables",
     )(*in_hbm(offsets, phase, y_table, x_table))
     groups = [[(chip * 2 + core) * NARROW + n for chip, n in SPOTS] for core in range(2)]
+    band = jnp.broadcast_to(band[None], (CHIPS,) + band.shape).reshape(len(SPOTS), 2 * YB, 128)
     mine = lax.all_to_all(band, ("wide", "narrow"), 0, 0, axis_index_groups=groups, tiled=True)
     mine, y_table, x_table, turn = lax.optimization_barrier((mine, y_table, x_table, turn))
     other = lax.ppermute(mine, "wide", [(i, i ^ 1) for i in range(2 * CHIPS)])

time: 46.6 us -> 47.1 us (1.011)
  local copies, waits for them, and re-layouts: 0 us -> 1.22 us
  Pallas kernels: 19.4 us -> 18.4 us
  starting transfers between devices: 15.2 us -> 15.7 us
    broadcast_in_dim x0 -> x1, local copies, waits for them, and re-layouts: none -> 1.22 us  [per_device(): jnp.broadcast_to(band[None], (CHIPS,) + band.shape)]
    pallas_call x1, Pallas kernels: 2.79 us -> 1.8 us  [per_device(): pl.pallas_call(band_kernel, out_shape=jax.ShapeDtypeStruct((NARROW, 2 * Y...]
    ppermute x1, starting transfers between devices: 1.35 us -> 1.93 us  [per_device(): other = lax.ppermute(mine, 'wide', [(i, i ^ 1) for i in range(2 * CHIPS)])]
where the time goes in v4:
time: 47.1 us; the launch traced here: 46.9 us
  Pallas kernels  18.4 us (39%)
  starting transfers between devices  15.7 us (33%)
  waiting for transfers between devices  11.5 us (24%)
  local copies, waits for them, and re-layouts  1.22 us (3%)
    all_to_all x1, starting transfers between devices, per_device(): lax.all_to_all(band, ('wide', 'narrow'), 0, 0, axis_index_groups=groups,...  13.7 us
    pallas_call x1, Pallas kernels, per_device(): pl.pallas_call(sample_kernel, out_shape=jax.ShapeDtypeStruct((SLABS, 2, S...  13.4 us
    all_to_all x1, waiting for transfers between devices, per_device(): lax.all_to_all(band, ('wide', 'narrow'), 0, 0, axis_index_groups=groups,...  10.8 us
    ppermute x1, starting transfers between devices, per_device(): other = lax.ppermute(mine, 'wide', [(i, i ^ 1) for i in range(2 * CHIPS)])  1.93 us
    pallas_call x1, Pallas kernels, per_device(): pl.pallas_call(band_kernel, out_shape=jax.ShapeDtypeStruct((NARROW, 2 * Y...  1.8 us
    pallas_call x1, Pallas kernels, per_device(): pl.pallas_call(table_kernel, out_shape=[jax.ShapeDtypeStruct((2 * G, 2 *...  1.66 us
    pallas_call x1, Pallas kernels, per_device(): pl.pallas_call(line_kernel, out_shape=jax.ShapeDtypeStruct((2, G * ZB, 12...  1.6 us
    broadcast_in_dim x1, local copies, waits for them, and re-layouts, per_device(): jnp.broadcast_to(band[None], (CHIPS,) + band.shape)  1.22 us
  transfers between devices with their start and end apart: 2, of which 2 were waited for; matrix products, arithmetic and copies ran while one was open for 0% of the time, Pallas kernels for 7%

profile of v4, /device:TPU:1, one launch (start us, length us, event | category | flops | bytes accessed | tf_op | source)
XLA Modules:
  0.0 46.9 jit_solution(11435324074280352678)
XLA Ops:
  0.0 1.8 %band.1 = bf16[8,64,128]{2,1,0:T(8,128)(2,1)S(1)} custom-call(f32[3,256]{1,0:T(4,128)} %scale_hbm.1, bf16[2,16,32,256]{3,2,1,0:T(8,128)(2,1)} %image_hbm.1, bf16[512,128]{1,0:T(8,128)(2,1)} %constant.15.z_hbm), custom_call_target="tpu_custom_call" | custom-call | tf_op jit(solution)/shard_map/band/pallas_call | solution.py:194
  1.8 1.2 %broadcast_in_dim.4 = bf16[8,8,64,128]{3,2,1,0:T(8,128)(2,1)} broadcast(bf16[8,64,128]{2,1,0:T(8,128)(2,1)S(1)} %band.1), dimensions={1,2,3} | broadcast | bytes 1179648 | tf_op jit(solution)/shard_map/broadcast_in_dim | solution.py:229
  3.0 13.7 %all-to-all-start = ((bf16[64,64,128]{2,1,0:T(8,128)(2,1)}), bf16[64,64,128]{2,1,0:T(8,128)(2,1)S(1)}, u32[]{:S(2)}, u32[]{:S(2)}) async-start(bf16[64,64,128]{2,1,0:T(8,128)(2,1)} %bitcast), calls=%async_computation | async-start | bytes 2097152 | tf_op jit(solution)/shard_map/all_to_all | solution.py:230
  16.8 1.7 %tables.1 = (bf16[1024,512]{1,0:T(8,128)(2,1)S(1)}, bf16[512,512]{1,0:T(8,128)(2,1)S(1)}, f32[16,512]{1,0:T(8,128)S(1)}) custom-call(s32[1,16]{1,0:T(1,128)} %offsets_hbm.1, f32[264,512]{1,0:T(8,128)} %constant.11.clone.phase_hbm, bf16[1024,512]{1,0:T(8,128)(2,1)} %constant.16.y_hbm, bf16[512,512]{1,0:T(8,128)(2,1)} %constant.17.x_hbm), custom_call_target="tpu_custom_call" | custom-call | tf_op jit(solution)/shard_map/tables/pallas_call | solution.py:210
  18.4 10.8 %all-to-all-done.source = bf16[64,64,128]{2,1,0:T(8,128)(2,1)S(1)} async-done(((bf16[64,64,128]{2,1,0:T(8,128)(2,1)}), bf16[64,64,128]{2,1,0:T(8,128)(2,1)S(1)}, u32[]{:S(2)}, u32[]{:S(2)}) %all-to-all-start) | async-done | bytes 1048608 | tf_op jit(solution)/shard_map/all_to_all | solution.py:230
  29.3 1.9 %collective-permute-start = (bf16[64,64,128]{2,1,0:T(8,128)(2,1)S(1)}, bf16[64,64,128]{2,1,0:T(8,128)(2,1)S(1)}, u32[]{:S(2)}, u32[]{:S(2)}) collective-permute-start(bf16[64,64,128]{2,1,0:T(8,128)(2,1)S(1)} %all-to-all-done.source), channel_id=1, source_target_pairs={{0,8},{8,0},{16,24},{24,16},{32,40},{40,32},{48,56},{56,48},{64,72... | collective-permute-start | bytes 3145736 | tf_op jit(solution)/shard_map/ppermute | solution.py:232
  31.2 1.6 %lines.1.own = f32[2,4096,128]{2,1,0:T(8,128)S(1)} custom-call(bf16[64,64,128]{2,1,0:T(8,128)(2,1)S(1)} %all-to-all-done.source, bf16[1024,512]{1,0:T(8,128)(2,1)S(1)} %get-tuple-element.16.y_table), custom_call_target="tpu_custom_call" | custom-call | flops 1073741824 | bytes 6291456 | tf_op jit(solution)/shard_map/lines/pallas_call | solution.py:233
  32.8 0.7 %collective-permute-done.other = bf16[64,64,128]{2,1,0:T(8,128)(2,1)S(1)} collective-permute-done((bf16[64,64,128]{2,1,0:T(8,128)(2,1)S(1)}, bf16[64,64,128]{2,1,0:T(8,128)(2,1)S(1)}, u32[]{:S(2)}, u32[]{:S(2)}) %collective-permute-start) | collective-permute-done | bytes 1048608 | tf_op jit(solution)/shard_map/ppermute | solution.py:232
  33.5 13.4 %samples.1 = f32[16,2,1536]{2,1,0:T(2,128)} custom-call(f32[2,4096,128]{2,1,0:T(8,128)S(1)} %lines.1.own, bf16[64,64,128]{2,1,0:T(8,128)(2,1)S(1)} %collective-permute-done.other, bf16[1024,512]{1,0:T(8,128)(2,1)S(1)} %get-tuple-element.16.y_table, bf16[512,512]{1,0:T(8,128)(2,1)S(1)} %get-tuple-element.17.x_table, f32[16,512]{1,0:T(8,128)S(1)} %get-tuple-element.18.turn, ...), custom_call_target="tpu_custom_call" | custom-call | tf_op jit(solution)/shard_map/samples/pallas_call | solution.py:243
Async XLA Ops:
  3.0 26.2 %all-to-all-start = ((bf16[64,64,128]{2,1,0:T(8,128)(2,1)}), bf16[64,64,128]{2,1,0:T(8,128)(2,1)S(1)}, u32[]{:S(2)}, u32[]{:S(2)}) async-start(bf16[64,64,128]{2,1,0:T(8,128)(2,1)} %bitcast), calls=%async_computation | async-start | bytes 2097152 | tf_op jit(solution)/shard_map/all_to_all | solution.py:230
  29.3 4.2 %collective-permute-start = (bf16[64,64,128]{2,1,0:T(8,128)(2,1)S(1)}, bf16[64,64,128]{2,1,0:T(8,128)(2,1)S(1)}, u32[]{:S(2)}, u32[]{:S(2)}) collective-permute-start(bf16[64,64,128]{2,1,0:T(8,128)(2,1)S(1)} %all-to-all-done.source), channel_id=1, source_target_pairs={{0,8},{8,0},{16,24},{24,16},{32,40},{40,32},{48,56},{56,48},{64,72... | collective-permute-start | bytes 3145736 | tf_op jit(solution)/shard_map/ppermute | solution.py:232

commit v5 on v3

--- a/solution.py
+++ b/solution.py
@@ -51,7 +51,7 @@
 
 def exchange_order():
     spots = [(x, y, z) for x in range(4) for y in range(4) for z in range(4)][::-1]
-    spots = spots[16:] + spots[:16]
+    spots = spots[8:] + spots[:8]
     return [(x // 2 * 4 + y, z * 2 + x % 2) for x, y, z in spots]
 
 

time: 46.6 us -> 46.9 us (level)
  waiting for transfers between devices: 11.7 us -> 12.7 us
  starting transfers between devices: 15.2 us -> 14.4 us
    all_to_all x1, starting transfers between devices: 13.9 us -> 12.7 us  [per_device(): lax.all_to_all(band, ('wide', 'narrow'), 0, 0, axis_index_groups=groups,...]
    all_to_all x1, waiting for transfers between devices: 11 us -> 12 us  [per_device(): lax.all_to_all(band, ('wide', 'narrow'), 0, 0, axis_index_groups=groups,...]
where the time goes in v5:
time: 46.9 us; the launch traced here: 46.6 us
  Pallas kernels  19.4 us (41%)
  starting transfers between devices  14.4 us (31%)
  waiting for transfers between devices  12.7 us (27%)
    pallas_call x1, Pallas kernels, per_device(): pl.pallas_call(sample_kernel, out_shape=jax.ShapeDtypeStruct((SLABS, 2, S...  13.4 us
    all_to_all x1, starting transfers between devices, per_device(): lax.all_to_all(band, ('wide', 'narrow'), 0, 0, axis_index_groups=groups,...  12.7 us
    all_to_all x1, waiting for transfers between devices, per_device(): lax.all_to_all(band, ('wide', 'narrow'), 0, 0, axis_index_groups=groups,...  12 us
    pallas_call x1, Pallas kernels, per_device(): pl.pallas_call(band_kernel, out_shape=jax.ShapeDtypeStruct((len(SPOTS), 2...  2.79 us
    ppermute x1, starting transfers between devices, per_device(): other = lax.ppermute(mine, 'wide', [(i, i ^ 1) for i in range(2 * CHIPS)])  1.69 us
    pallas_call x1, Pallas kernels, per_device(): pl.pallas_call(table_kernel, out_shape=[jax.ShapeDtypeStruct((2 * G, 2 *...  1.66 us
    pallas_call x1, Pallas kernels, per_device(): pl.pallas_call(line_kernel, out_shape=jax.ShapeDtypeStruct((2, G * ZB, 12...  1.6 us
  transfers between devices with their start and end apart: 2, of which 2 were waited for; matrix products, arithmetic and copies ran while one was open for 0% of the time, Pallas kernels for 7%

profile of v5, /device:TPU:1, one launch (start us, length us, event | category | flops | bytes accessed | tf_op | source)
XLA Modules:
  0.0 46.6 jit_solution(5221151703153272187)
XLA Ops:
  0.0 2.8 %band.1 = bf16[64,64,128]{2,1,0:T(8,128)(2,1)} custom-call(f32[3,256]{1,0:T(4,128)} %scale_hbm.1, bf16[2,16,32,256]{3,2,1,0:T(8,128)(2,1)} %image_hbm.1, bf16[512,128]{1,0:T(8,128)(2,1)} %constant.15.z_hbm), custom_call_target="tpu_custom_call" | custom-call | tf_op jit(solution)/shard_map/band/pallas_call | solution.py:201
  2.8 12.7 %all-to-all-start = ((bf16[64,64,128]{2,1,0:T(8,128)(2,1)}), bf16[64,64,128]{2,1,0:T(8,128)(2,1)S(1)}, u32[]{:S(2)}, u32[]{:S(2)}) async-start(bf16[64,64,128]{2,1,0:T(8,128)(2,1)} %band.1), calls=%async_computation | async-start | bytes 2097152 | tf_op jit(solution)/shard_map/all_to_all | solution.py:236
  15.5 1.7 %tables.1 = (bf16[1024,512]{1,0:T(8,128)(2,1)S(1)}, bf16[512,512]{1,0:T(8,128)(2,1)S(1)}, f32[16,512]{1,0:T(8,128)S(1)}) custom-call(s32[1,16]{1,0:T(1,128)} %offsets_hbm.1, f32[264,512]{1,0:T(8,128)} %constant.11.clone.phase_hbm, bf16[1024,512]{1,0:T(8,128)(2,1)} %constant.16.y_hbm, bf16[512,512]{1,0:T(8,128)(2,1)} %constant.17.x_hbm), custom_call_target="tpu_custom_call" | custom-call | tf_op jit(solution)/shard_map/tables/pallas_call | solution.py:217
  17.2 12.0 %all-to-all-done.source = bf16[64,64,128]{2,1,0:T(8,128)(2,1)S(1)} async-done(((bf16[64,64,128]{2,1,0:T(8,128)(2,1)}), bf16[64,64,128]{2,1,0:T(8,128)(2,1)S(1)}, u32[]{:S(2)}, u32[]{:S(2)}) %all-to-all-start) | async-done | bytes 1048608 | tf_op jit(solution)/shard_map/all_to_all | solution.py:236
  29.3 1.7 %collective-permute-start = (bf16[64,64,128]{2,1,0:T(8,128)(2,1)S(1)}, bf16[64,64,128]{2,1,0:T(8,128)(2,1)S(1)}, u32[]{:S(2)}, u32[]{:S(2)}) collective-permute-start(bf16[64,64,128]{2,1,0:T(8,128)(2,1)S(1)} %all-to-all-done.source), channel_id=1, source_target_pairs={{0,8},{8,0},{16,24},{24,16},{32,40},{40,32},{48,56},{56,48},{64,72... | collective-permute-start | bytes 3145736 | tf_op jit(solution)/shard_map/ppermute | solution.py:238
  30.9 1.6 %lines.1.own = f32[2,4096,128]{2,1,0:T(8,128)S(1)} custom-call(bf16[64,64,128]{2,1,0:T(8,128)(2,1)S(1)} %all-to-all-done.source, bf16[1024,512]{1,0:T(8,128)(2,1)S(1)} %get-tuple-element.16.y_table), custom_call_target="tpu_custom_call" | custom-call | flops 1073741824 | bytes 6291456 | tf_op jit(solution)/shard_map/lines/pallas_call | solution.py:239
  32.6 0.7 %collective-permute-done.other = bf16[64,64,128]{2,1,0:T(8,128)(2,1)S(1)} collective-permute-done((bf16[64,64,128]{2,1,0:T(8,128)(2,1)S(1)}, bf16[64,64,128]{2,1,0:T(8,128)(2,1)S(1)}, u32[]{:S(2)}, u32[]{:S(2)}) %collective-permute-start) | collective-permute-done | bytes 1048608 | tf_op jit(solution)/shard_map/ppermute | solution.py:238
  33.2 13.4 %samples.1 = f32[16,2,1536]{2,1,0:T(2,128)} custom-call(f32[2,4096,128]{2,1,0:T(8,128)S(1)} %lines.1.own, bf16[64,64,128]{2,1,0:T(8,128)(2,1)S(1)} %collective-permute-done.other, bf16[1024,512]{1,0:T(8,128)(2,1)S(1)} %get-tuple-element.16.y_table, bf16[512,512]{1,0:T(8,128)(2,1)S(1)} %get-tuple-element.17.x_table, f32[16,512]{1,0:T(8,128)S(1)} %get-tuple-element.18.turn, ...), custom_call_target="tpu_custom_call" | custom-call | tf_op jit(solution)/shard_map/samples/pallas_call | solution.py:249
Async XLA Ops:
  2.8 26.5 %all-to-all-start = ((bf16[64,64,128]{2,1,0:T(8,128)(2,1)}), bf16[64,64,128]{2,1,0:T(8,128)(2,1)S(1)}, u32[]{:S(2)}, u32[]{:S(2)}) async-start(bf16[64,64,128]{2,1,0:T(8,128)(2,1)} %band.1), calls=%async_computation | async-start | bytes 2097152 | tf_op jit(solution)/shard_map/all_to_all | solution.py:236
  29.3 4.0 %collective-permute-start = (bf16[64,64,128]{2,1,0:T(8,128)(2,1)S(1)}, bf16[64,64,128]{2,1,0:T(8,128)(2,1)S(1)}, u32[]{:S(2)}, u32[]{:S(2)}) collective-permute-start(bf16[64,64,128]{2,1,0:T(8,128)(2,1)S(1)} %all-to-all-done.source), channel_id=1, source_target_pairs={{0,8},{8,0},{16,24},{24,16},{32,40},{40,32},{48,56},{56,48},{64,72... | collective-permute-start | bytes 3145736 | tf_op jit(solution)/shard_map/ppermute | solution.py:238
